TPU v7x, 256 devices: a whole 4x4x8 slice. The times are simulated.
256 devices in a mesh: dp: 32 (over y, x, core), tensor: 8 (over z).
Axes of the slice: x: 4, y: 4, z: 8, core: 2. Of those that a mesh axis runs over, the one named last changes fastest.
Arguments:
- text: bfloat16 [32, 256, 5120], P('dp', None, 'tensor'), may hold values from -6 to 6
- prompts: bfloat16 [32, 100, 5120], P('dp', None, 'tensor'), may hold values from -6 to 6
- gain: float32 [5120], replicated, may hold values from 0.1 to 1.9
- w_query: bfloat16 [5120, 3072], P(None, 'tensor'), may hold values from -0.069877124 to 0.069877124, as said below
- w_key: bfloat16 [5120, 3072], P(None, 'tensor'), may hold values from -1.2577882 to 1.2577882, as said below
- w_value: bfloat16 [5120, 3072], P(None, 'tensor'), may hold values from -0.078125 to 0.078125
- cotangent: bfloat16 [32, 356, 3072], P('dp', None, 'tensor'), may hold values from -6 to 6
- task_of: int32 [32], replicated, may hold values from 0 to 31, as said below
- lengths: int32 [32], replicated, may hold values from 1 to 256, as said below
- slot: int32 [32], replicated, may hold values from 0 to 31, as said below
Outputs:
- attn_out: bfloat16 [32, 356, 3072], P('dp', None, 'tensor')
- prompt_grad: float32 [32, 100, 5120], P('dp', None, 'tensor')
Inputs may be any that keep to these rules, and one draw needn't show every extreme that they name: `task_of`: nondecreasing along the source order. `lengths`: some example has exactly 256 text tokens; rows of an example beyond its length are padding. `slot`: a permutation of 0 to 31; position s lies on index s // 1 of dp. `w_query`: entries of order 5120 ** -0.5. `w_key`: entries of order 5120 ** -0.5 or larger.
All inputs are finite; a program needn't handle non-finite values.
Results may differ from a plain program's by a relative error of at most 0.0082.
Values may be sent and summed in bfloat16 or wider, within the bound.
A program may use at most 128 MiB of HBM per device.

v0:
```python
import math

import jax
import jax.numpy as jnp
from jax import lax
from jax.sharding import PartitionSpec as P

HD = 128


def in_one_piece(arrays, axis, split_dim, concat_dim, along):
    widths = [a.shape[along] for a in arrays]
    both = jnp.concatenate(arrays, axis=along)
    result = lax.all_to_all(both, axis, split_axis=split_dim, concat_axis=concat_dim, tiled=True)
    return tuple(jnp.split(result, [sum(widths[:k]) for k in range(1, len(widths))], axis=along))


def cut_along(value, dim, peers):
    before, after = (value.shape[:dim], value.shape[dim + 1 :])
    return jnp.moveaxis(value.reshape(*before, peers, -1, *after), dim, 0)


def sent_and_summed(value, axis, dim):
    pieces = cut_along(value, dim, lax.axis_size(axis))
    arrived = lax.all_to_all(pieces, axis, split_axis=0, concat_axis=0, tiled=True)
    return arrived.astype(jnp.float32).sum(axis=0)


def rope_tables(row_count):
    half_dim = HD // 2
    frequency = 10000.0 ** (-jnp.arange(half_dim, dtype=jnp.float32) / half_dim)
    angle_table = jnp.arange(row_count, dtype=jnp.float32)[:, None] * frequency[None, :]
    return (jnp.cos(angle_table), jnp.sin(angle_table))


def rotate(vectors, cosine_table, sine_table):
    half_dim = vectors.shape[-1] // 2
    first_half = vectors[..., :half_dim]
    second_half = vectors[..., half_dim:]
    cosine_b = cosine_table[:, None, :]
    sine_b = sine_table[:, None, :]
    return jnp.concatenate(
        [
            first_half * cosine_b - second_half * sine_b,
            second_half * cosine_b + first_half * sine_b,
        ],
        axis=-1,
    )


def unrotate(vectors, cosine_table, sine_table):
    half_dim = vectors.shape[-1] // 2
    first_half = vectors[..., :half_dim]
    second_half = vectors[..., half_dim:]
    cosine_b = cosine_table[:, None, :]
    sine_b = sine_table[:, None, :]
    return jnp.concatenate(
        [
            first_half * cosine_b + second_half * sine_b,
            second_half * cosine_b - first_half * sine_b,
        ],
        axis=-1,
    )


def transpose_product(grad_low, matrix):
    return lax.dot_general(
        grad_low, matrix, (((1,), (1,)), ((), ())), preferred_element_type=jnp.float32
    )


def attention_window(full_rows, gain, w_query, w_key, w_value, cotangent, valid_rows, prompt_len):
    batch_size, row_count, model_width = full_rows.shape
    head_count = w_query.shape[1] // HD
    wide_rows = full_rows.astype(jnp.float32)
    inv_rms = lax.rsqrt(jnp.mean(wide_rows * wide_rows, axis=-1) + 1e-05)
    normed = (
        (wide_rows * inv_rms[..., None] * gain)
        .astype(jnp.bfloat16)
        .reshape(batch_size * row_count, model_width)
    )
    cosine_table, sine_table = rope_tables(row_count)

    def project(matrix):
        return jnp.dot(normed, matrix, preferred_element_type=jnp.float32).reshape(
            batch_size, row_count, head_count, HD
        )

    queries = rotate(project(w_query), cosine_table, sine_table).astype(jnp.bfloat16)
    key_rows = rotate(project(w_key), cosine_table, sine_table).astype(jnp.bfloat16)
    value_rows = project(w_value).astype(jnp.bfloat16)
    score_scale = 1.0 / math.sqrt(HD)
    scores = (
        jnp.einsum("erhd,ekhd->ehrk", queries, key_rows, preferred_element_type=jnp.float32)
        * score_scale
    )
    rows_at = jnp.arange(row_count, dtype=jnp.int32)
    row_limit = prompt_len + valid_rows
    allowed = (rows_at[None, None, :] <= rows_at[None, :, None]) & (
        rows_at[None, None, :] < row_limit[:, None, None]
    )
    allowed = allowed[:, None]
    scores = jnp.where(allowed, scores, -1e30)
    row_peak = jnp.max(scores, axis=-1, keepdims=True)
    weights = jnp.where(allowed, jnp.exp(scores - row_peak), 0.0)
    probability = weights / jnp.sum(weights, axis=-1, keepdims=True)
    probs_low = probability.astype(jnp.bfloat16)
    live_rows = rows_at[None, :] < row_limit[:, None]
    mixed_rows = jnp.einsum(
        "ehrk,ekhd->erhd", probs_low, value_rows, preferred_element_type=jnp.float32
    )
    mixed_rows = jnp.where(live_rows[:, :, None, None], mixed_rows, 0.0)
    output = mixed_rows.reshape(batch_size, row_count, head_count * HD).astype(jnp.bfloat16)
    upstream = jnp.where(
        live_rows[:, :, None, None], cotangent.reshape(batch_size, row_count, head_count, HD), 0.0
    )
    grad_prob = jnp.einsum(
        "erhd,ekhd->ehrk", upstream, value_rows, preferred_element_type=jnp.float32
    )
    row_delta = jnp.sum(probability * grad_prob, axis=-1, keepdims=True)
    grad_score = (probability * (grad_prob - row_delta)).astype(jnp.bfloat16)
    grad_query = (
        jnp.einsum(
            "ehrk,ekhd->erhd",
            grad_score[:, :, :prompt_len, :],
            key_rows,
            preferred_element_type=jnp.float32,
        )
        * score_scale
    )
    grad_key = (
        jnp.einsum(
            "ehrk,erhd->ekhd",
            grad_score[:, :, :, :prompt_len],
            queries,
            preferred_element_type=jnp.float32,
        )
        * score_scale
    )
    grad_value = jnp.einsum(
        "ehrk,erhd->ekhd",
        probs_low[:, :, :, :prompt_len],
        upstream,
        preferred_element_type=jnp.float32,
    )
    cosine_lead = cosine_table[:prompt_len]
    sine_lead = sine_table[:prompt_len]
    flat_rows = batch_size * prompt_len
    grad_query = (
        unrotate(grad_query, cosine_lead, sine_lead)
        .astype(jnp.bfloat16)
        .reshape(flat_rows, head_count * HD)
    )
    grad_key = (
        unrotate(grad_key, cosine_lead, sine_lead)
        .astype(jnp.bfloat16)
        .reshape(flat_rows, head_count * HD)
    )
    grad_value = grad_value.astype(jnp.bfloat16).reshape(flat_rows, head_count * HD)
    grad_normed = (
        transpose_product(grad_query, w_query)
        + transpose_product(grad_key, w_key)
        + transpose_product(grad_value, w_value)
    )
    grad_normed = grad_normed.reshape(batch_size, prompt_len, model_width) * gain
    prompt_rows = wide_rows[:, :prompt_len]
    prompt_inv = inv_rms[:, :prompt_len, None]
    grad_rows = prompt_inv * grad_normed - prompt_rows * prompt_inv**3 * jnp.mean(
        grad_normed * prompt_rows, axis=-1, keepdims=True
    )
    return (output, grad_rows)


def on_device(text, prompts, gain, w_query, w_key, w_value, cotangent, task_of, lengths, slot):
    dp_count = lax.axis_size("dp")
    my_index = lax.axis_index("dp")
    ex_dev = text.shape[0]
    task_dev = prompts.shape[0]
    prompt_len = prompts.shape[1]
    example_count = slot.shape[0]
    task_count = task_dev * dp_count
    places = jnp.arange(example_count, dtype=jnp.int32)
    matching = slot[None, :] == places[:, None]
    task_slot = jnp.sum(jnp.where(matching, task_of[None, :], 0), axis=1)
    length_slot = jnp.sum(jnp.where(matching, lengths[None, :], 0), axis=1)
    first_place = my_index * ex_dev
    my_lengths = lax.dynamic_slice_in_dim(length_slot, first_place, ex_dev)
    task_ids = jnp.arange(task_count, dtype=jnp.int32)
    spread_text, spread_prompts = in_one_piece((text, prompts), "dp", 2, 0, 1)
    taking = matching.astype(jnp.bfloat16)
    placed_text = jnp.einsum(
        "se,erc->src", taking, spread_text, preferred_element_type=jnp.bfloat16
    )
    choosing = (task_slot[:, None] == task_ids[None, :]).astype(jnp.bfloat16)
    placed_prompts = jnp.einsum(
        "st,tpc->spc", choosing, spread_prompts, preferred_element_type=jnp.bfloat16
    )
    placed = jnp.concatenate([placed_prompts, placed_text], axis=1)
    placed = placed.reshape(dp_count, ex_dev, placed.shape[1], placed.shape[2])
    local_rows = lax.all_to_all(placed, "dp", split_axis=0, concat_axis=3, tiled=True)[0]
    full_rows = lax.all_gather(local_rows, "tensor", axis=2, tiled=True)
    output, grad_part = attention_window(
        full_rows, gain, w_query, w_key, w_value, cotangent, my_lengths, prompt_len
    )
    grad_share = sent_and_summed(grad_part.astype(jnp.bfloat16), "tensor", 2)
    spread_grads = lax.all_to_all(
        grad_share.astype(jnp.bfloat16), "dp", split_axis=2, concat_axis=0, tiled=True
    ).astype(grad_share.dtype)
    collecting = (task_ids[:, None] == task_slot[None, :]).astype(jnp.float32)
    per_task = jnp.einsum("ts,spc->tpc", collecting, spread_grads, precision=lax.Precision.HIGHEST)
    prompt_grad = lax.all_to_all(
        per_task.astype(jnp.bfloat16), "dp", split_axis=0, concat_axis=2, tiled=True
    ).astype(per_task.dtype)
    return (output, prompt_grad)


def solution(mesh):
    in_specs = (
        P("dp", None, "tensor"),
        P("dp", None, "tensor"),
        P(),
        P(None, "tensor"),
        P(None, "tensor"),
        P(None, "tensor"),
        P("dp", None, "tensor"),
        P(),
        P(),
        P(),
    )
    out_specs = (P("dp", None, "tensor"), P("dp", None, "tensor"))
    return jax.shard_map(
        on_device, mesh=mesh, in_specs=in_specs, out_specs=out_specs, check_vma=False
    )
```

profile of v0, /device:TPU:1, one launch (start us, length us, event | category | flops | bytes accessed | tf_op | source)
XLA Modules:
  0.0 210.7 jit_solution(12513714038176524248)
XLA Ops:
  7.2 1.1 pad_maximum_fusion
  8.3 1.5 copy.62
  9.8 0.5 broadcast.175
  10.3 3.8 %reduce.14 = bf16[640,356]{1,0:T(8,128)(2,1)S(1)} reduce(bf16[640,1,356]{2,1,0:T(2,128)(2,1)S(1)} %bitcast.165, bf16[]{:T(256)} %broadcast.175), dimensions={1}, to_apply=%bitcast.137.reduce_sub_computation | reduce | bytes 911362
  14.1 1.5 reshape.387
  15.6 8.6 %all-to-all-start = ((bf16[32,2,3560]{2,1,0:T(2,128)(2,1)}), bf16[32,2,3560]{2,1,0:T(2,128)(2,1)S(1)}, u32[]{:S(2)}, u32[]{:S(2)}) async-start(bf16[32,2,3560]{2,1,0:T(2,128)(2,1)} %reshape.387), calls=%async_computation | async-start | bytes 917504 | tf_op jit(solution)/shard_map/all_to_all | solution.py:14
  24.4 10.6 %all-to-all-done = bf16[32,2,3560]{2,1,0:T(2,128)(2,1)S(1)} async-done(((bf16[32,2,3560]{2,1,0:T(2,128)(2,1)}), bf16[32,2,3560]{2,1,0:T(2,128)(2,1)S(1)}, u32[]{:S(2)}, u32[]{:S(2)}) %all-to-all-start) | async-done | bytes 455712 | tf_op jit(solution)/shard_map/all_to_all | solution.py:14
  35.0 1.0 reshape.388
  36.0 2.8 %bitcast_reduce_fusion = bf16[356,640]{0,1:T(8,128)(2,1)S(1)} fusion(bf16[640,1,356]{2,1,0:T(2,128)(2,1)S(1)} %reshape.388), kind=kLoop, calls=%fused_computation.102 | loop fusion | bytes 911360 | tf_op jit(solution)/shard_map/all_to_all | solution.py:14
  39.1 0.2 fusion.21
  39.3 0.2 fusion.30
  39.5 0.2 maximum_bitcast_fusion
  39.8 0.2 copy.64
  40.0 15.7 %all_to_all.65 = bf16[32,1,356,20]{2,3,1,0:T(8,128)(2,1)S(1)} all-to-all(bf16[32,1,356,20]{2,3,1,0:T(8,128)(2,1)S(1)} %copy.64), channel_id=1, replica_groups=mesh['dp'=32,'tensor'=8] {'dp'}, dimensions={0} | all-to-all | bytes 911360 | tf_op jit(solution)/shard_map/all_to_all | solution.py:200
  55.6 0.2 squeeze.3
  55.9 1.0 copy.65
  56.9 0.2 copy.71
  57.1 0.7 fusion.29
  57.9 6.3 %copy.67 = bf16[5120,384]{0,1:T(8,128)(2,1)} copy(bf16[5120,384]{1,0:T(8,128)(2,1)} %param.13) | data formatting | bytes 7864320 | tf_op args[3]
  64.1 6.3 %copy.68 = bf16[5120,384]{0,1:T(8,128)(2,1)} copy(bf16[5120,384]{1,0:T(8,128)(2,1)} %param.14) | data formatting | bytes 7864320 | tf_op args[4]
  70.4 6.3 %copy.66 = bf16[5120,384]{0,1:T(8,128)(2,1)} copy(bf16[5120,384]{1,0:T(8,128)(2,1)} %param.15) | data formatting | bytes 7864320 | tf_op args[5]
  76.7 0.6 dynamic_slice.3
  78.1 27.9 %all-gather.2.cloned.1.call-done = bf16[1,356,5120]{2,1,0:T(8,128)(2,1)} async-done(((bf16[1,356,640]{2,1,0:T(8,128)(2,1)}), bf16[1,356,5120]{2,1,0:T(8,128)(2,1)}) %all-gather.2.cloned.1.call-update) | async-done | bytes 3645456 | tf_op jit(solution)/shard_map/all_gather | solution.py:201
  105.9 3.0 %multiply_reduce_fusion = f32[356]{0:T(512)S(1)} fusion(bf16[1,356,5120]{2,1,0:T(8,128)(2,1)} %all-gather.2.cloned.1.call-done), kind=kLoop, calls=%fused_computation.3 | loop fusion | flops 5467804 | bytes 3646864 | tf_op jit(solution)/shard_map/reduce_sum | solution.py:76
  109.0 0.5 multiply_multiply_fusion
  109.5 0.6 slice_bitcast_fusion.7
  110.1 4.5 %convolution_bitcast_fusion.2 = f32[1,356,3,128]{3,1,2,0:T(8,128)S(1)} fusion(bf16[3,128,5120]{2,1,0:T(8,128)(2,1)} %bitcast.164, f32[5120]{0:T(1024)S(1)} %copy-done.9, f32[356]{0:T(512)S(1)} %add_rsqrt_fusion, bf16[1,356,5120]{2,1,0:T(8,128)(2,1)S(1)} %copy-done.3), kind=kOutput, calls=%fused_computation.21 | convolution fusion | flops 1407139840 | bytes 8146320 | tf_op jit(solution)/shard_map/dot_general | solution.py:85
  114.6 2.3 %convolution_bitcast_fusion.1 = f32[1,356,3,128]{3,1,2,0:T(8,128)S(1)} fusion(bf16[3,128,5120]{2,1,0:T(8,128)(2,1)S(1)} %bitcast.163, f32[5120]{0:T(1024)S(1)} %copy-done.9, f32[356]{0:T(512)S(1)} %add_rsqrt_fusion, bf16[1,356,5120]{2,1,0:T(8,128)(2,1)S(1)} %copy-done.3), kind=kOutput, calls=%fused_computation.20 | convolution fusion | flops 1407139840 | bytes 8146320 | tf_op jit(solution)/shard_map/dot_general | solution.py:85
  117.0 0.5 fusion.23
  117.4 1.1 fusion.53
  118.5 0.1 convert_bitcast_fusion
  118.6 5.4 %convolution_convert_fusion = bf16[356,3,128]{2,0,1:T(8,128)(2,1)S(1)} fusion(bf16[3,128,5120]{2,1,0:T(8,128)(2,1)} %bitcast.162, f32[5120]{0:T(1024)S(1)} %copy-done.9, f32[356]{0:T(512)S(1)} %add_rsqrt_fusion, bf16[1,356,5120]{2,1,0:T(8,128)(2,1)} %all-gather.2.cloned.1.call-done), kind=kOutput, calls=%fused_computation.22 | convolution fusion | flops 1407276544 | bytes 7872912 | tf_op jit(solution)/shard_map/dot_general | solution.py:85
  124.1 0.4 fusion.27
  124.5 0.5 fusion.10
  125.1 0.3 fusion.16
  125.4 0.4 fusion.17
  125.8 0.3 fusion.18
  126.2 0.2 add_convert_fusion.2
  126.8 1.2 copy-done.1
  127.9 1.7 fusion.54
  129.6 0.4 copy-done
  130.0 1.9 convolution_add_fusion.1
  132.1 0.9 convert_element_type.106
  133.0 1.2 copy-done.2
  134.2 1.9 fusion.4
  136.1 0.5 fusion.5
  136.6 0.1 copy.95
  137.0 31.2 %all_to_all.66 = bf16[8,1,100,640]{3,2,1,0:T(8,128)(2,1)S(1)} all-to-all(bf16[8,1,100,640]{3,2,1,0:T(8,128)(2,1)S(1)} %bitcast.159), channel_id=1, replica_groups=mesh['dp'=32,'tensor'=8] {'tensor'}, dimensions={0} | all-to-all | bytes 2048000 | tf_op jit(solution)/shard_map/all_to_all | solution.py:25
  168.2 0.2 reduce_sum.74
  168.4 0.2 copy.80
  168.6 1.7 reduce.15
  170.3 0.2 reshape.389
  170.5 17.0 %all_to_all.67 = bf16[32,2,1000]{2,1,0:T(2,128)(2,1)S(1)} all-to-all(bf16[32,2,1000]{2,1,0:T(2,128)(2,1)S(1)} %reshape.389), channel_id=1, replica_groups=mesh['dp'=32,'tensor'=8] {'dp'}, dimensions={0} | all-to-all | bytes 256000 | tf_op jit(solution)/shard_map/all_to_all | solution.py:206
  187.5 0.3 reshape.390
  187.8 1.0 bitcast_reduce_fusion.1
  188.8 0.2 convolution_convert_fusion.1
  189.0 0.7 copy.82
  189.8 3.9 %all-to-all-start.4 = ((bf16[32,100,20]{1,2,0:T(8,128)(2,1)}), bf16[32,100,20]{1,2,0:T(8,128)(2,1)S(1)}, u32[]{:S(2)}, u32[]{:S(2)}) async-start(bf16[32,100,20]{1,2,0:T(8,128)(2,1)} %copy.82), calls=%async_computation.4 | async-start | bytes 393216 | tf_op jit(solution)/shard_map/all_to_all | solution.py:211
  193.7 0.5 fusion.15
  194.3 0.2 copy.70
  194.5 0.9 copy.83
  195.4 6.7 %all-to-all-done.4 = bf16[32,100,20]{1,2,0:T(8,128)(2,1)S(1)} async-done(((bf16[32,100,20]{1,2,0:T(8,128)(2,1)}), bf16[32,100,20]{1,2,0:T(8,128)(2,1)S(1)}, u32[]{:S(2)}, u32[]{:S(2)}) %all-to-all-start.4) | async-done | bytes 128032 | tf_op jit(solution)/shard_map/all_to_all | solution.py:211
  202.1 0.3 reshape.379
  202.4 1.4 copy.84
  (62 shorter events, 1.4 us)
Async XLA Ops:
  8.3 16.0 %copy-start.12 = (s32[32]{0:T(128)S(1)}, s32[32]{0:T(128)}, u32[]{:S(2)}) copy-start(s32[32]{0:T(128)} %param.19) | copy-start | bytes 388
  8.3 16.0 %copy-start.17 = (s32[32]{0:T(128)S(1)}, s32[32]{0:T(128)}, u32[]{:S(2)}) copy-start(s32[32]{0:T(128)} %param.18) | copy-start | bytes 388
  8.3 16.0 %copy-start.18 = (s32[32]{0:T(128)S(1)}, s32[32]{0:T(128)}, u32[]{:S(2)}) copy-start(s32[32]{0:T(128)} %param.17) | copy-start | bytes 388
  15.6 19.4 %all-to-all-start = ((bf16[32,2,3560]{2,1,0:T(2,128)(2,1)}), bf16[32,2,3560]{2,1,0:T(2,128)(2,1)S(1)}, u32[]{:S(2)}, u32[]{:S(2)}) async-start(bf16[32,2,3560]{2,1,0:T(2,128)(2,1)} %reshape.387), calls=%async_computation | async-start | bytes 917504 | tf_op jit(solution)/shard_map/all_to_all | solution.py:14
  24.2 81.7 %all-gather.2.cloned.1.call-start = ((), (), s32[]{:S(2)}) async-start(), calls=%async_computation.5 | async-start | bytes 4147200 | tf_op jit(solution)/shard_map/all_gather | solution.py:201
  39.8 17.1 %copy-start.6 = (bf16[1,356,384]{2,1,0:T(8,128)(2,1)S(1)}, bf16[1,356,384]{2,1,0:T(8,128)(2,1)}, u32[]{:S(2)}) copy-start(bf16[1,356,384]{2,1,0:T(8,128)(2,1)} %param.16) | copy-start | bytes 820228
  76.7 33.4 %copy-start.9 = (f32[5120]{0:T(1024)S(1)}, f32[5120]{0:T(1024)}, u32[]{:S(2)}) copy-start(f32[5120]{0:T(1024)} %param.12) | copy-start | bytes 61444
  77.9 28.0 %copy-start.13 = (pred[356]{0:T(512)(128)(4,1)}, pred[356]{0:T(512)(128)(4,1)S(1)}, u32[]{:S(2)}) copy-start(pred[356]{0:T(512)(128)(4,1)S(1)} %iota_compare_fusion.4) | copy-start | bytes 1072
  105.9 4.1 %copy-start.3 = (bf16[1,356,5120]{2,1,0:T(8,128)(2,1)S(1)}, bf16[1,356,5120]{2,1,0:T(8,128)(2,1)}, u32[]{:S(2)}) copy-start(bf16[1,356,5120]{2,1,0:T(8,128)(2,1)} %all-gather.2.cloned.1.call-done) | copy-start | bytes 10936324
  110.1 4.6 %copy-start.5 = (bf16[5120,384]{0,1:T(8,128)(2,1)S(1)}, bf16[5120,384]{0,1:T(8,128)(2,1)}, u32[]{:S(2)}) copy-start(bf16[5120,384]{0,1:T(8,128)(2,1)} %copy.68) | copy-start | bytes 11796484
  118.5 6.0 %copy-start.10 = (f32[3,356]{1,0:T(4,128)}, f32[3,356]{1,0:T(4,128)S(1)}, u32[]{:S(2)}) copy-start(f32[3,356]{1,0:T(4,128)S(1)} %get-tuple-element.24) | copy-start | bytes 12820
  118.6 5.4 %copy-start.14 = (pred[356]{0:T(512)(128)(4,1)S(1)}, pred[356]{0:T(512)(128)(4,1)}, u32[]{:S(2)}) copy-start(pred[356]{0:T(512)(128)(4,1)} %copy-done.13) | copy-start | bytes 1072
  124.1 1.0 copy-start.7
  125.8 2.1 %copy-start.1 = (bf16[5120,384]{1,0:T(8,128)(2,1)S(1)}, bf16[5120,384]{1,0:T(8,128)(2,1)}, u32[]{:S(2)}) copy-start(bf16[5120,384]{1,0:T(8,128)(2,1)} %param.13) | copy-start | bytes 11796484
  127.9 2.1 %copy-start = (bf16[5120,384]{1,0:T(8,128)(2,1)S(1)}, bf16[5120,384]{1,0:T(8,128)(2,1)}, u32[]{:S(2)}) copy-start(bf16[5120,384]{1,0:T(8,128)(2,1)} %param.14) | copy-start | bytes 11796484
  130.0 2.0 copy-start.4
  132.1 2.1 %copy-start.2 = (bf16[5120,384]{1,0:T(8,128)(2,1)S(1)}, bf16[5120,384]{1,0:T(8,128)(2,1)}, u32[]{:S(2)}) copy-start(bf16[5120,384]{1,0:T(8,128)(2,1)} %param.15) | copy-start | bytes 11796484
  134.2 1.9 copy-start.15
  134.2 1.9 copy-start.16
  168.4 25.3 %copy-start.8 = (bf16[356,3,128]{2,0,1:T(8,128)(2,1)S(1)}, bf16[356,3,128]{2,0,1:T(8,128)(2,1)}, u32[]{:S(2)}) copy-start(bf16[356,3,128]{2,0,1:T(8,128)(2,1)} %copy-done.7) | copy-start | bytes 820228
  168.4 25.3 %copy-start.11 = (f32[3,356]{1,0:T(4,128)S(1)}, f32[3,356]{1,0:T(4,128)}, u32[]{:S(2)}) copy-start(f32[3,356]{1,0:T(4,128)} %copy-done.10) | copy-start | bytes 12820
  189.8 12.3 %all-to-all-start.4 = ((bf16[32,100,20]{1,2,0:T(8,128)(2,1)}), bf16[32,100,20]{1,2,0:T(8,128)(2,1)S(1)}, u32[]{:S(2)}, u32[]{:S(2)}) async-start(bf16[32,100,20]{1,2,0:T(8,128)(2,1)} %copy.82), calls=%async_computation.4 | async-start | bytes 393216 | tf_op jit(solution)/shard_map/all_to_all | solution.py:211
Sparse Core Ops, SparseCore 0:
  57.0 48.8 all-gather.1
where the time goes:
time: 212 us; the launch traced here: 211 us
  blocking collectives  63.8 us (30%)
  waiting for transfers between devices  45.1 us (21%)
  local copies, waits for them, and re-layouts  38.2 us (18%)
  matrix products  21.4 us (10%)
  between operations  15.3 us (7%)
  other arithmetic  14.3 us (7%)
  starting transfers between devices  12.5 us (6%)
    all_to_all x1, blocking collectives, sent_and_summed(): lax.all_to_all(pieces, axis, split_axis=0, concat_axis=0, tiled=True)  31.2 us
    unnamed x56, local copies, waits for them, and re-layouts  28.3 us
    all_gather x1, waiting for transfers between devices, on_device(): full_rows = lax.all_gather(local_rows, 'tensor', axis=2, tiled=True)  27.9 us
    all_to_all x1, blocking collectives, on_device(): lax.all_to_all(grad_share.astype(jnp.bfloat16), 'dp', split_axis=2, conca...  17 us
    all_to_all x1, blocking collectives, on_device(): lax.all_to_all(placed, 'dp', split_axis=0, concat_axis=3, tiled=True)[0]  15.7 us
    dot_general x3, matrix products, project(): jnp.dot(normed, matrix, preferred_element_type=jnp.float32)  12.3 us
    all_to_all x1, waiting for transfers between devices, in_one_piece(): lax.all_to_all(both, axis, split_axis=split_dim, concat_axis=concat_dim,...  10.6 us
    all_to_all x1, starting transfers between devices, in_one_piece(): lax.all_to_all(both, axis, split_axis=split_dim, concat_axis=concat_dim,...  8.58 us
  transfers between devices with their start and end apart: 3, of which 3 were waited for; matrix products, arithmetic and copies ran while one was open for 11% of the time, Pallas kernels for 0%

commit v1 on v0

v1 whole, which is shorter than its diff:
```python
import math

import jax
import jax.numpy as jnp
import numpy as np
from jax import lax
from jax.experimental import pallas as pl
from jax.experimental.pallas import tpu as pltpu
from jax.sharding import PartitionSpec as P

HD = 128
HALF = 64
EPS = 1e-05
MESH = pl.DeviceIdType.MESH
BF = jnp.bfloat16
F32 = jnp.float32

TEXT = 256
PROMPT = 100
PROMPT_PAD = 128
PROMPT_SENT = 104
ROWS = TEXT + PROMPT
ROWS_PAD = TEXT + PROMPT_PAD
COLS = 640
TILES = COLS // 128
HEADS = 3
WIDTH = HEADS * HD
ALL = 3 * WIDTH
NZ = 8
ND = 32
G_PIECES = 20
R_PIECES = 23
TEXT_SUB = 4
SUBS = ((0, 64), (64, 64), (128, 64), (192, 64), (0, 56), (56, 48))
LAST = ((0, 1, 4), (2, 3, 5))
RS_LAST = ((0, 1, 2), (3, 4))
T_TASK, T_SLOT, T_INV, T_LAST, T_HAS, T_SAME, T_LEN = range(7)


def rope_constants():
    frequency = (np.float32(10000.0) ** (-np.arange(HALF, dtype=np.float32) / np.float32(HALF))).astype(np.float32)
    position = np.concatenate([np.arange(TEXT) + PROMPT, np.arange(PROMPT_PAD)]).astype(np.float32)
    angle = (position[:, None] * frequency[None, :]).astype(np.float32)
    cosine = np.cos(angle.astype(np.float64)).astype(np.float32)
    sine = np.sin(angle.astype(np.float64)).astype(np.float32)
    return np.concatenate([cosine, cosine], axis=1), np.concatenate([-sine, sine], axis=1)


def dot(a, b):
    return lax.dot_general(a, b, (((1,), (0,)), ((), ())), preferred_element_type=F32)


def dot_t(a, b):
    return lax.dot_general(a, b, (((1,), (1,)), ((), ())), preferred_element_type=F32)


def kernel(
    tab, text_hbm, prompts_hbm, gain, wq_hbm, wk_hbm, wv_hbm, cot_hbm, cos_hbm, sin_hbm,
    out_ref, pg_ref,
    text_all, prm_all, pr_loc, ct_loc, w_all, cos_t, sin_t, acc, nb, inv_t, inv_p, s_col,
    sst_all, ssp_all, sx_all,
    pp_src, pp_mid, pp_send, pp_dst,
    ct_src, ct_mid, ct_send, ct_dst,
    ot_src, ot_mid, ot_send, ot_dst,
    gr_src, gr_mid, gr_send, gr_dst, gr_run,
    u_ext, u_t, u_p, o_full, gcat, rs_tx, rs_rx,
    local_sem, ag_s, ag_r, rs_s, rs_r, sm_s, sm_r, a2_s, a2_r,
):
    d = lax.axis_index("dp")
    z = lax.axis_index("tensor")

    def mod8(v):
        return lax.rem(v + 16, NZ)

    loads = [
        pltpu.make_async_copy(prompts_hbm.at[0], pr_loc, local_sem.at[0]),
        pltpu.make_async_copy(text_hbm.at[0], text_all.at[z], local_sem.at[1]),
        pltpu.make_async_copy(cot_hbm.at[0], ct_loc, local_sem.at[2]),
        pltpu.make_async_copy(wq_hbm, w_all.at[:, pl.ds(0, WIDTH)], local_sem.at[3]),
        pltpu.make_async_copy(wk_hbm, w_all.at[:, pl.ds(WIDTH, WIDTH)], local_sem.at[4]),
        pltpu.make_async_copy(wv_hbm, w_all.at[:, pl.ds(2 * WIDTH, WIDTH)], local_sem.at[5]),
        pltpu.make_async_copy(cos_hbm, cos_t, local_sem.at[6]),
        pltpu.make_async_copy(sin_hbm, sin_t, local_sem.at[7]),
    ]
    for load in loads:
        load.start()

    barrier = pltpu.get_barrier_semaphore()

    def greet_dp(i, carry):
        pl.semaphore_signal(barrier, inc=1, device_id={"dp": lax.rem(d + i, ND)}, device_id_type=MESH)
        return carry

    def greet_z(i, carry):
        pl.semaphore_signal(barrier, inc=1, device_id={"tensor": lax.rem(z + i, NZ)}, device_id_type=MESH)
        return carry

    lax.fori_loop(1, NZ, greet_z, 0)
    lax.fori_loop(1, ND, greet_dp, 0)

    def remote(src, dst, s_sem, r_sem, where):
        return pltpu.make_async_remote_copy(
            src_ref=src, dst_ref=dst, send_sem=s_sem, recv_sem=r_sem, device_id=where, device_id_type=MESH
        )

    def middle(pieces):
        mine = lax.div(d * pieces + ND - 1, ND)
        there = jnp.logical_and(mine < pieces, lax.div(mine * ND, pieces) == d)
        return mine, there

    def scatter_one(src, mid, pieces, which, p):
        m = lax.div(p * ND, pieces) if not isinstance(p, int) else (p * ND) // pieces

        @pl.when(m != d)
        def _():
            remote(src.at[p], mid.at[d], a2_s.at[which, 0], a2_r.at[which, 0], {"dp": m}).start()

        @pl.when(m == d)
        def _():
            mid[d] = src[p]

    def scatter(src, mid, pieces, which):
        def body(i, carry):
            scatter_one(src, mid, pieces, which, lax.rem(d + i, pieces))
            return carry

        lax.fori_loop(0, pieces, body, 0)

    def await_middle(mid, which):
        part = mid.at[pl.ds(0, ND - 1)]
        pltpu.make_async_copy(part, part, a2_r.at[which, 0]).wait()

    def relay(value, send, dst, which, mine):
        def body(i, carry):
            e = lax.rem(d + i, ND)
            send[e] = value(e)

            @pl.when(e != d)
            def _():
                remote(send.at[e], dst.at[mine], a2_s.at[which, 1], a2_r.at[which, 1], {"dp": e}).start()

            @pl.when(e == d)
            def _():
                dst[mine] = send[e]

            return carry

        lax.fori_loop(0, ND, body, 0)

    def await_pieces(dst, sem, pieces, there):
        @pl.when(there)
        def _():
            part = dst.at[pl.ds(0, pieces - 1)]
            pltpu.make_async_copy(part, part, sem).wait()

        @pl.when(jnp.logical_not(there))
        def _():
            part = dst.at[pl.ds(0, pieces)]
            pltpu.make_async_copy(part, part, sem).wait()

    def finish_sends(src, send, pieces, which, there):
        await_pieces(src, a2_s.at[which, 0], pieces, there)

        @pl.when(there)
        def _():
            part = send.at[pl.ds(0, ND - 1)]
            pltpu.make_async_copy(part, part, a2_s.at[which, 1]).wait()

    mine_g, there_g = middle(G_PIECES)
    mine_r, there_r = middle(R_PIECES)
    PP, CT, OT, GR = range(4)

    def send_small(ref, which):
        def body(i, carry):
            remote(ref.at[z], ref.at[z], sm_s.at[which], sm_r.at[which], {"tensor": lax.rem(z + i, NZ)}).start()
            return carry

        lax.fori_loop(1, NZ, body, 0)

    def await_small(ref, sem):
        part = ref.at[pl.ds(0, NZ - 1)]
        pltpu.make_async_copy(part, part, sem).wait()

    SIGN = (1, -1)

    def ring_rows(c, j):
        first, count = SUBS[j]
        return (text_all if j < TEXT_SUB else prm_all).at[c, pl.ds(first, count), :]

    def ring_send(way, k, j):
        rows = ring_rows(mod8(z - SIGN[way] * (k - 1)), j)
        return remote(rows, rows, ag_s.at[way, k - 1, j], ag_r.at[way, k - 1, j], {"tensor": mod8(z + SIGN[way])})

    def ring_recv(way, k, j):
        rows = ring_rows(mod8(z - SIGN[way] * k), j)
        return remote(rows, rows, ag_s.at[way, k - 1, j], ag_r.at[way, k - 1, j], {"tensor": mod8(z + SIGN[way])})

    def ring_step(k, subs):
        for j in subs:
            for way in range(2):
                ring_recv(way, k, j).wait_recv()
                if j in LAST[way]:
                    ring_send(way, k + 1, j).start()
                else:

                    @pl.when(k < 3)
                    def _(way=way, j=j):
                        ring_send(way, k + 1, j).start()

    loads[0].wait()
    for c in range(TILES):
        lanes = slice(128 * c, 128 * c + 128)
        for g in range(3):
            pp_src[g * TILES + c] = pr_loc[32 * g : 32 * g + 32, lanes]
        pp_src[3 * TILES + c] = jnp.zeros((32, 128), BF)
        pp_src[3 * TILES + c, 0:4] = pr_loc[96:100, lanes]
        gr_src[3 * TILES + c] = jnp.zeros((32, 128), BF)
    loads[1].wait()
    total = jnp.zeros((TEXT, 128), F32)
    for c in range(TILES):
        x = text_all[z, :, 128 * c : 128 * c + 128].astype(F32)
        total = total + x * x
    sums = jnp.broadcast_to(jnp.sum(total, axis=1, keepdims=True), (TEXT, 128))
    sst_all[z] = sums.T[0:1]
    pl.semaphore_wait(barrier, ND - 1 + NZ - 1)

    for j in range(TEXT_SUB):
        for way in range(2):
            ring_send(way, 1, j).start()
    scatter(pp_src, pp_mid, G_PIECES, PP)
    send_small(sst_all, 0)

    loads[2].wait()
    for p in range(R_PIECES - 1):
        ct_src[p] = ct_loc[16 * p : 16 * p + 16]
    ct_src[R_PIECES - 1] = jnp.zeros((16, WIDTH), BF)
    ct_src[R_PIECES - 1, 0:4] = ct_loc[352:356]
    prm_all[:, PROMPT_SENT:, :] = jnp.zeros((NZ, PROMPT_PAD - PROMPT_SENT, COLS), BF)

    @pl.when(there_g)
    def _():
        await_middle(pp_mid, PP)
        relay(lambda e: pp_mid[tab[T_TASK, e]], pp_send, pp_dst, PP, mine_g)

    scatter(ct_src, ct_mid, R_PIECES, CT)
    acc[...] = jnp.zeros_like(acc)

    ring_step(1, range(TEXT_SUB))
    await_pieces(pp_dst, a2_r.at[PP, 1], G_PIECES, there_g)
    for g in range(4):
        for c in range(TILES):
            prm_all[z, 32 * g : 32 * g + 32, 128 * c : 128 * c + 128] = pp_dst[g * TILES + c]
    for j in range(TEXT_SUB, len(SUBS)):
        for way in range(2):
            ring_send(way, 1, j).start()
    total = jnp.zeros((PROMPT_PAD, 128), F32)
    for c in range(TILES):
        x = prm_all[z, :, 128 * c : 128 * c + 128].astype(F32)
        total = total + x * x
    sums = jnp.broadcast_to(jnp.sum(total, axis=1, keepdims=True), (PROMPT_PAD, 128))
    ssp_all[z] = sums.T[0:1]
    send_small(ssp_all, 1)

    @pl.when(there_r)
    def _():
        await_middle(ct_mid, CT)
        relay(lambda e: ct_mid[tab[T_SLOT, e]], ct_send, ct_dst, CT, mine_r)

    def inverse(ref, rows):
        squares = ref[0]
        for i in range(1, NZ):
            squares = squares + ref[i]
        inv = lax.rsqrt(squares * (1.0 / (NZ * COLS)) + EPS)
        return jnp.broadcast_to(inv, (128, rows)).T

    await_small(sst_all, sm_r.at[0])
    inv_t[...] = inverse(sst_all, TEXT)
    await_small(ssp_all, sm_r.at[1])
    inv_p[...] = inverse(ssp_all, PROMPT_PAD)

    def project(c):
        for t in range(TILES):
            lanes = slice(128 * t, 128 * t + 128)
            scale = gain[c, :, lanes]
            nb[0:TEXT, lanes] = (text_all[c, :, lanes].astype(F32) * inv_t[...] * scale).astype(BF)
            nb[TEXT:, lanes] = (prm_all[c, :, lanes].astype(F32) * inv_p[...] * scale).astype(BF)
        rows = pl.ds(pl.multiple_of(c * COLS, COLS), COLS)
        for n in range(3):
            wide = slice(WIDTH * n, WIDTH * n + WIDTH)
            acc[:, wide] += dot(nb[...], w_all[rows, wide])

    def project_each(k, count):
        def body(i, carry):
            project(mod8(z + k * (i - 1) if count == 3 else z + k * (2 * i - 1)))
            return carry

        lax.fori_loop(0, count, body, 0)

    ring_step(1, range(TEXT_SUB, len(SUBS)))
    for load in loads[3:6]:
        load.wait()
    project_each(1, 3)

    def middle_steps(k, carry):
        ring_step(k, range(len(SUBS)))
        project_each(k, 2)
        return carry

    lax.fori_loop(2, 4, middle_steps, 0)

    length = tab[T_LEN, d]
    await_pieces(ct_dst, a2_r.at[CT, 1], R_PIECES, there_r)
    for p in range(R_PIECES):
        u_ext[16 * p : 16 * p + 16] = ct_dst[p].astype(F32)
    u_ext[16 * R_PIECES :] = jnp.zeros((ROWS_PAD - 16 * R_PIECES, WIDTH), F32)
    text_row = lax.broadcasted_iota(jnp.int32, (TEXT, 128), 0)
    prompt_row = lax.broadcasted_iota(jnp.int32, (PROMPT_PAD, 128), 0)
    for h in range(HEADS):
        lanes = slice(HD * h, HD * h + HD)
        x = u_ext[:, lanes]
        shifted = pltpu.roll(x, ROWS_PAD - PROMPT, 0)
        u_t[:, lanes] = jnp.where(text_row < length, shifted[0:TEXT], 0.0).astype(BF)
        u_p[:, lanes] = jnp.where(prompt_row < PROMPT, x[0:PROMPT_PAD], 0.0).astype(BF)
    loads[6].wait()
    loads[7].wait()

    for way in range(2):
        for j in LAST[way]:
            ring_recv(way, 4, j).wait_recv()
    project(mod8(z + 4))

    score_scale = 1.0 / math.sqrt(HD)
    cos_all, sin_all = cos_t[...], sin_t[...]
    cos_p, sin_p = cos_all[TEXT:], sin_all[TEXT:]
    row_tt = lax.broadcasted_iota(jnp.int32, (TEXT, TEXT), 0)
    col_tt = lax.broadcasted_iota(jnp.int32, (TEXT, TEXT), 1)
    ok_tt = (col_tt <= row_tt) & (col_tt < length)
    ok_tp = lax.broadcasted_iota(jnp.int32, (TEXT, PROMPT_PAD), 1) < PROMPT
    row_pp = lax.broadcasted_iota(jnp.int32, (PROMPT_PAD, PROMPT_PAD), 0)
    col_pp = lax.broadcasted_iota(jnp.int32, (PROMPT_PAD, PROMPT_PAD), 1)
    ok_pp = (col_pp <= row_pp) & (col_pp < PROMPT)
    s_part = jnp.zeros((PROMPT_PAD, HD), F32)
    for h in range(HEADS):
        lanes = slice(HD * h, HD * h + HD)
        pre_q = acc[:, HD * h : HD * h + HD]
        pre_k = acc[:, WIDTH + HD * h : WIDTH + HD * h + HD]
        pre_v = acc[:, 2 * WIDTH + HD * h : 2 * WIDTH + HD * h + HD]
        q = (pre_q * cos_all + pltpu.roll(pre_q, HALF, 1) * sin_all).astype(BF)
        k = (pre_k * cos_all + pltpu.roll(pre_k, HALF, 1) * sin_all).astype(BF)
        v = pre_v.astype(BF)
        qt, qp, kt, kp, vt, vp = q[:TEXT], q[TEXT:], k[:TEXT], k[TEXT:], v[:TEXT], v[TEXT:]
        s_tt = jnp.where(ok_tt, dot_t(qt, kt) * score_scale, -1e30)
        s_tp = jnp.where(ok_tp, dot_t(qt, kp) * score_scale, -1e30)
        s_pp = jnp.where(ok_pp, dot_t(qp, kp) * score_scale, -1e30)
        peak = jnp.maximum(jnp.max(s_tt, axis=1, keepdims=True), jnp.max(s_tp, axis=1, keepdims=True))
        e_tt = jnp.where(ok_tt, jnp.exp(s_tt - peak), 0.0)
        e_tp = jnp.where(ok_tp, jnp.exp(s_tp - peak), 0.0)
        norm = 1.0 / (jnp.sum(e_tt, axis=1, keepdims=True) + jnp.sum(e_tp, axis=1, keepdims=True))
        p_tt, p_tp = e_tt * norm, e_tp * norm
        e_pp = jnp.where(ok_pp, jnp.exp(s_pp - jnp.max(s_pp, axis=1, keepdims=True)), 0.0)
        p_pp = e_pp * (1.0 / jnp.sum(e_pp, axis=1, keepdims=True))
        mixed = dot(p_tt.astype(BF), vt) + dot(p_tp.astype(BF), vp)
        o_full[0:TEXT, lanes] = jnp.where(text_row < length, mixed, 0.0)
        o_full[TEXT:, lanes] = dot(p_pp.astype(BF), vp)
        ut, up = u_t[:, lanes], u_p[:, lanes]
        d_tt, d_tp, d_pp = dot_t(ut, vt), dot_t(ut, vp), dot_t(up, vp)
        delta_t = jnp.sum(p_tt * d_tt, axis=1, keepdims=True) + jnp.sum(p_tp * d_tp, axis=1, keepdims=True)
        g_tp = p_tp * (d_tp - delta_t)
        g_pp = p_pp * (d_pp - jnp.sum(p_pp * d_pp, axis=1, keepdims=True))
        grad_q = dot(g_pp.astype(BF), kp) * score_scale
        grad_k = (dot(g_tp.T.astype(BF), qt) + dot(g_pp.T.astype(BF), qp)) * score_scale
        grad_v = (dot(p_tp.T.astype(BF), ut) + dot(p_pp.T.astype(BF), up)).astype(BF)
        grad_q = (grad_q * cos_p - pltpu.roll(grad_q, HALF, 1) * sin_p).astype(BF)
        grad_k = (grad_k * cos_p - pltpu.roll(grad_k, HALF, 1) * sin_p).astype(BF)
        gcat[:, HD * h : HD * h + HD] = grad_q
        gcat[:, WIDTH + HD * h : WIDTH + HD * h + HD] = grad_k
        gcat[:, 2 * WIDTH + HD * h : 2 * WIDTH + HD * h + HD] = grad_v
        s_part = s_part + grad_q.astype(F32) * pre_q[TEXT:] + grad_k.astype(F32) * pre_k[TEXT:]
        s_part = s_part + grad_v.astype(F32) * pre_v[TEXT:]

    def grad_block(j):
        rows = pl.ds(pl.multiple_of(j * COLS, COLS), COLS)
        return dot_t(gcat[0:PROMPT_SENT], w_all[rows, :])

    def rs_copy(way, step, t):
        return remote(
            rs_tx.at[way, step, t], rs_rx.at[way, step, t], rs_s.at[way, step, t], rs_r.at[way, step, t],
            {"tensor": mod8(z + SIGN[way])},
        )

    def rs_put(way, step, t, value):
        rs_tx[way, step, t] = value.astype(BF)
        rs_copy(way, step, t).start()

    block = grad_block(mod8(z + 4))
    for way in range(2):
        for t in RS_LAST[way]:
            rs_put(way, 0, t, block[:, 128 * t : 128 * t + 128])
    sx_all[z] = jnp.broadcast_to(jnp.sum(s_part, axis=1, keepdims=True), (PROMPT_PAD, 128)).T[0:1]
    send_small(sx_all, 2)

    for h in range(HEADS):
        lanes = slice(HD * h, HD * h + HD)
        x = o_full[:, lanes]
        head_row = lax.broadcasted_iota(jnp.int32, (ROWS_PAD, 128), 0)
        outer = jnp.where(head_row < PROMPT, jnp.concatenate([x[TEXT:], x[:TEXT]], axis=0), pltpu.roll(x, PROMPT, 0))
        outer = outer.astype(BF)
        for p in range(R_PIECES):
            ot_src[p, :, lanes] = outer[16 * p : 16 * p + 16]
    scatter(ot_src, ot_mid, R_PIECES, OT)

    for step in range(1, 4):
        blocks = (grad_block(mod8(z + 4 - step)), grad_block(mod8(z - 4 + step)))
        for t in range(TILES):
            for way in range(2):
                value = blocks[way][:, 128 * t : 128 * t + 128]
                if step > 1 or t in RS_LAST[way]:
                    rs_copy(way, step - 1, t).wait_recv()
                    value = value + rs_rx[way, step - 1, t].astype(F32)
                rs_put(way, step, t, value)
        if step == 2:

            @pl.when(there_r)
            def _():
                await_middle(ot_mid, OT)
                relay(lambda s: ot_mid[tab[T_INV, s]], ot_send, ot_dst, OT, mine_r)

    own = grad_block(z)
    await_small(sx_all, sm_r.at[2])
    total = sx_all[0]
    for i in range(1, NZ):
        total = total + sx_all[i]
    s_col[...] = jnp.broadcast_to(total * (1.0 / (NZ * COLS)), (128, PROMPT_PAD)).T
    inv = inv_p[0:PROMPT_SENT]
    second = inv * inv * s_col[0:PROMPT_SENT]
    for t in range(TILES):
        lanes = slice(128 * t, 128 * t + 128)
        value = own[:, lanes]
        for way in range(2):
            rs_copy(way, 3, t).wait_recv()
            value = value + rs_rx[way, 3, t].astype(F32)
        value = inv * (value * gain[z, :, lanes]) - prm_all[z, 0:PROMPT_SENT, lanes].astype(F32) * second
        value = value.astype(BF)
        for g in range(4):
            p = g * TILES + t
            if g < 3:
                gr_src[p] = value[32 * g : 32 * g + 32]
            else:
                gr_src[p, 0:8] = value[96:104]
            scatter_one(gr_src, gr_mid, G_PIECES, GR, p)

    @pl.when(there_g)
    def _():
        await_middle(gr_mid, GR)

        def run(e, before):
            now = gr_mid[e].astype(F32) + jnp.where(tab[T_SAME, e] > 0, before, 0.0)
            gr_run[e] = now
            return now

        lax.fori_loop(0, ND, run, jnp.zeros((32, 128), F32))
        relay(
            lambda t: jnp.where(tab[T_HAS, t] > 0, gr_run[tab[T_LAST, t]], 0.0).astype(BF),
            gr_send, gr_dst, GR, mine_g,
        )

    await_pieces(ot_dst, a2_r.at[OT, 1], R_PIECES, there_r)
    for p in range(R_PIECES - 1):
        out_ref[0, 16 * p : 16 * p + 16] = ot_dst[p]
    out_ref[0, 352:356] = ot_dst[R_PIECES - 1, 0:4]

    await_pieces(gr_dst, a2_r.at[GR, 1], G_PIECES, there_g)
    for c in range(TILES):
        lanes = slice(128 * c, 128 * c + 128)
        for g in range(3):
            pg_ref[0, 32 * g : 32 * g + 32, lanes] = gr_dst[g * TILES + c].astype(F32)
        pg_ref[0, 96:100, lanes] = gr_dst[3 * TILES + c, 0:4].astype(F32)

    finish_sends(pp_src, pp_send, G_PIECES, PP, there_g)
    finish_sends(ct_src, ct_send, R_PIECES, CT, there_r)
    finish_sends(ot_src, ot_send, R_PIECES, OT, there_r)
    finish_sends(gr_src, gr_send, G_PIECES, GR, there_g)
    await_small(sst_all, sm_s.at[0])
    await_small(ssp_all, sm_s.at[1])
    await_small(sx_all, sm_s.at[2])
    for way in range(2):
        for j in range(len(SUBS)):
            for k in range(1, 5):
                if k < 4 or j in LAST[way]:
                    ring_send(way, k, j).wait_send()
        for step in range(4):
            for t in range(TILES):
                if step > 0 or t in RS_LAST[way]:
                    rs_copy(way, step, t).wait_send()


def on_device(text, prompts, gain, w_query, w_key, w_value, cotangent, task_of, lengths, slot):
    order = jnp.arange(ND, dtype=jnp.int32)
    inverse = jnp.sum(jnp.where(slot[None, :] == order[:, None], order[None, :], 0), axis=1)
    upto = jnp.sum((task_of[None, :] <= order[:, None]).astype(jnp.int32), axis=1)
    here = jnp.sum((task_of[None, :] == order[:, None]).astype(jnp.int32), axis=1)
    same = jnp.concatenate([jnp.zeros((1,), jnp.int32), (task_of[1:] == task_of[:-1]).astype(jnp.int32)])
    table = jnp.stack([task_of, slot, inverse, jnp.maximum(upto - 1, 0), here, same, lengths, lengths])
    cosine, sine = rope_constants()
    vmem, dma = pltpu.VMEM, pltpu.SemaphoreType.DMA
    anywhere = pl.BlockSpec(memory_space=pl.ANY)
    whole = pl.BlockSpec(memory_space=pltpu.VMEM)
    g_piece, r_piece = (32, 128), (16, WIDTH)
    return pl.pallas_call(
        kernel,
        out_shape=(
            jax.ShapeDtypeStruct((1, ROWS, WIDTH), BF),
            jax.ShapeDtypeStruct((1, PROMPT, COLS), F32),
        ),
        in_specs=[pl.BlockSpec(memory_space=pltpu.SMEM), anywhere, anywhere, whole] + [anywhere] * 6,
        out_specs=(whole, whole),
        scratch_shapes=[
            vmem((NZ, TEXT, COLS), BF), vmem((NZ, PROMPT_PAD, COLS), BF), vmem((PROMPT, COLS), BF),
            vmem((ROWS, WIDTH), BF), vmem((NZ * COLS, ALL), BF),
            vmem((ROWS_PAD, HD), F32), vmem((ROWS_PAD, HD), F32),
            vmem((ROWS_PAD, ALL), F32), vmem((ROWS_PAD, COLS), BF),
            vmem((TEXT, 128), F32), vmem((PROMPT_PAD, 128), F32), vmem((PROMPT_PAD, 128), F32),
            vmem((NZ, 1, TEXT), F32), vmem((NZ, 1, PROMPT_PAD), F32), vmem((NZ, 1, PROMPT_PAD), F32),
            vmem((G_PIECES, *g_piece), BF), vmem((ND, *g_piece), BF), vmem((ND, *g_piece), BF), vmem((G_PIECES, *g_piece), BF),
            vmem((R_PIECES, *r_piece), BF), vmem((ND, *r_piece), BF), vmem((ND, *r_piece), BF), vmem((R_PIECES, *r_piece), BF),
            vmem((R_PIECES, *r_piece), BF), vmem((ND, *r_piece), BF), vmem((ND, *r_piece), BF), vmem((R_PIECES, *r_piece), BF),
            vmem((G_PIECES, *g_piece), BF), vmem((ND, *g_piece), BF), vmem((ND, *g_piece), BF), vmem((G_PIECES, *g_piece), BF),
            vmem((ND, *g_piece), F32),
            vmem((ROWS_PAD, WIDTH), F32), vmem((TEXT, WIDTH), BF), vmem((PROMPT_PAD, WIDTH), BF),
            vmem((ROWS_PAD, WIDTH), F32), vmem((PROMPT_PAD, ALL), BF),
            vmem((2, 4, TILES, PROMPT_SENT, 128), BF), vmem((2, 4, TILES, PROMPT_SENT, 128), BF),
            dma((8,)), dma((2, 4, len(SUBS))), dma((2, 4, len(SUBS))), dma((2, 4, TILES)), dma((2, 4, TILES)),
            dma((3,)), dma((3,)), dma((4, 2)), dma((4, 2)),
        ],
        compiler_params=pltpu.CompilerParams(
            collective_id=0, has_side_effects=True, vmem_limit_bytes=60 * 1024 * 1024
        ),
    )(
        table, text, prompts, gain.reshape(NZ, 1, COLS), w_query, w_key, w_value, cotangent,
        jnp.asarray(cosine), jnp.asarray(sine),
    )


def solution(mesh):
    in_specs = (
        P("dp", None, "tensor"),
        P("dp", None, "tensor"),
        P(),
        P(None, "tensor"),
        P(None, "tensor"),
        P(None, "tensor"),
        P("dp", None, "tensor"),
        P(),
        P(),
        P(),
    )
    out_specs = (P("dp", None, "tensor"), P("dp", None, "tensor"))
    return jax.shard_map(on_device, mesh=mesh, in_specs=in_specs, out_specs=out_specs, check_vma=False)
```

time: 212 us -> 94.9 us (0.45)
  Pallas kernels: 0 us -> 86.7 us
  blocking collectives: 63.8 us -> 0 us
  waiting for transfers between devices: 45.1 us -> 0 us
  local copies, waits for them, and re-layouts: 38.2 us -> 4.94 us
  matrix products: 21.4 us -> 0 us
  between operations: 15.3 us -> 0.64 us
  starting transfers between devices: 12.5 us -> 0 us
  other arithmetic: 14.3 us -> 2.43 us
    pallas_call x0 -> x1, Pallas kernels: none -> 86.7 us  [on_device(): pl.pallas_call(kernel, out_shape=(jax.ShapeDtypeStruct((1, ROWS, WIDTH),...]
    all_to_all x3 -> x0, blocking collectives: 63.8 us -> none  [the longest x1 31.2 us: sent_and_summed(): lax.all_to_all(pieces, axis, split_axis=0, concat_axis=0, tiled=True)]
    all_gather x1 -> x0, waiting for transfers between devices: 27.9 us -> none  [on_device(): full_rows = lax.all_gather(local_rows, 'tensor', axis=2, tiled=True)]
    unnamed x56 -> x1, local copies, waits for them, and re-layouts: 28.3 us -> 1.69 us
    dot_general x14 -> x0, matrix products: 20.4 us -> none  [the longest x3 12.3 us: project(): jnp.dot(normed, matrix, preferred_element_type=jnp.float32)]
    all_to_all x2 -> x0, waiting for transfers between devices: 17.3 us -> none  [the longest x1 10.6 us: in_one_piece(): lax.all_to_all(both, axis, split_axis=split_dim, concat_axis=concat_dim,...]
    all_to_all x2 -> x0, starting transfers between devices: 12.5 us -> none  [the longest x1 8.58 us: in_one_piece(): lax.all_to_all(both, axis, split_axis=split_dim, concat_axis=concat_dim,...]
    unnamed x2 -> x0, other arithmetic: 5.44 us -> none
  transfers between devices with their start and end apart: 3 -> 0, of which waited for: 3 -> 0; matrix products, arithmetic and copies ran while one was open for 11% -> 0% of each run, Pallas kernels for 0% -> 0%
where the time goes in v1:
time: 94.9 us; the launch traced here: 94.7 us
  Pallas kernels  86.7 us (91%)
  local copies, waits for them, and re-layouts  4.94 us (5%)
  other arithmetic  2.43 us (3%)
    pallas_call x1, Pallas kernels, on_device(): pl.pallas_call(kernel, out_shape=(jax.ShapeDtypeStruct((1, ROWS, WIDTH),...  86.7 us
    pallas_call x1, local copies, waits for them, and re-layouts, on_device(): pl.pallas_call(kernel, out_shape=(jax.ShapeDtypeStruct((1, ROWS, WIDTH),...  1.91 us

profile of v1, /device:TPU:1, one launch (start us, length us, event | category | flops | bytes accessed | tf_op | source)
XLA Modules:
  0.0 94.7 jit_solution(17428441296696006350)
XLA Ops:
  0.6 0.8 select_reduce_fusion
  1.4 0.8 slice_compare_fusion
  2.2 0.1 fusion
  2.3 0.8 convert_reduce_fusion
  3.1 1.3 %stack.33.tab = s32[8,32]{1,0:T(8,128)} concatenate(s32[1,32]{1,0:T(1,128)} %bitcast.13, s32[1,32]{1,0:T(1,128)} %bitcast.14, s32[1,32]{1,0:T(1,128)S(1)} %bitcast.15, s32[1,32]{1,0:T(1,128)S(1)} %maximum_bitcast_fusion, s32[1,32]{1,0:T(1,128)S(1)} %bitcast.16, s32[1,32]{1,0:T(1,128)S(1)} %fusion, s32[1,32]{1,0:T(1,128)} %bitcast.11, s32[1,32]{1,0:T(1,128)} %bitcast.12), dimensions={0} | concatenate | bytes 2048 | tf_op jit(solution)/shard_map/stack | solution.py:503
  4.4 86.7 %shard_map.131 = (bf16[1,356,384]{2,1,0:T(8,128)(2,1)}, f32[1,100,640]{2,1,0:T(8,128)}) custom-call(s32[8,32]{1,0:T(8,128)} %stack.33.tab, bf16[1,256,640]{2,1,0:T(8,128)(2,1)} %text_hbm.1, bf16[1,100,640]{2,1,0:T(8,128)(2,1)} %prompts_hbm.1, f32[8,1,640]{2,1,0:T(1,128)} %bitcast.10, bf16[5120,384]{1,0:T(8,128)(2,1)} %wq_hbm.1, bf16[5120,384]{1,0:T(8,128)(2,1)} %wk_hbm.1, ...), custom_call_target="tpu_custom_call" | custom-call | tf_op jit(solution)/shard_map/pallas_call | solution.py:509
  91.1 1.9 %copy.15 = f32[1,100,640]{2,0,1:T(1,128)} copy(f32[1,100,640]{2,1,0:T(8,128)} %get-tuple-element.5) | data formatting | bytes 512000 | tf_op jit(solution)/shard_map/pallas_call | solution.py:509
  93.0 1.7 %copy.17 = bf16[1,356,384]{2,1,0:T(8,128)(2,1)} copy(bf16[1,356,384]{2,1,0:T(8,128)(2,1)} %get-tuple-element.10) | data formatting | bytes 546816
  (1 shorter events, 0.0 us)

commit v2 on v1

v2 whole, which is shorter than its diff:
```python
import math

import jax
import jax.numpy as jnp
import numpy as np
from jax import lax
from jax.experimental import pallas as pl
from jax.experimental.pallas import tpu as pltpu
from jax.sharding import PartitionSpec as P

HD = 128
HALF = 64
EPS = 1e-05
MESH = pl.DeviceIdType.MESH
BF = jnp.bfloat16
F32 = jnp.float32

TEXT = 256
PROMPT = 100
PROMPT_PAD = 128
PROMPT_SENT = 104
ROWS = TEXT + PROMPT
ROWS_PAD = TEXT + PROMPT_PAD
COLS = 640
TILES = COLS // 128
HEADS = 3
WIDTH = HEADS * HD
ALL = 3 * WIDTH
NZ = 8
ND = 32
G_ROWS = 16
G_HIGH = 6
R_ROWS = 40
R_HIGH = 9
R_PIECES = HEADS * R_HIGH
TEXT_SUB = 4
SUBS = ((0, 64), (64, 64), (128, 64), (192, 64), (0, 56), (56, 48))
LAST = ((0, 1, 4), (2, 3, 5))
RS_LAST = ((0, 1, 2), (3, 4))
RS_ORDER = ((3, 4, 0, 1, 2), (0, 1, 2, 3, 4))


def rope_constants():
    frequency = (np.float32(10000.0) ** (-np.arange(HALF, dtype=np.float32) / np.float32(HALF))).astype(np.float32)
    position = np.concatenate([np.arange(TEXT) + PROMPT, np.arange(PROMPT_PAD)]).astype(np.float32)
    angle = (position[:, None] * frequency[None, :]).astype(np.float32)
    cosine = np.cos(angle.astype(np.float64)).astype(np.float32)
    sine = np.sin(angle.astype(np.float64)).astype(np.float32)
    return np.concatenate([cosine, cosine], axis=1), np.concatenate([-sine, sine], axis=1)


def dot(a, b):
    return lax.dot_general(a, b, (((1,), (0,)), ((), ())), preferred_element_type=F32)


def dot_t(a, b):
    return lax.dot_general(a, b, (((1,), (1,)), ((), ())), preferred_element_type=F32)


def tail_rows(tiles):
    last = jnp.concatenate(tiles + [jnp.zeros((12, 128), F32)], axis=0)
    return last[0:16], last[16:32]


def kernel(
    task_of, lengths, slot, text_hbm, prompts_hbm, gain, wq_hbm, wk_hbm, wv_hbm, cot_hbm, cos_hbm, sin_hbm,
    ot_dst, gr_dst,
    inverse_slot, last_of,
    text_all, prm_all, pr_loc, ct_loc, w_all, cos_t, sin_t, acc, nb, inv_t, inv_p, s_col,
    sst_all, ssp_all, spt_all, sx_all,
    pp_src, pp_mid, pp_send, pp_dst,
    ct_src, ct_mid, ct_send, ct_dst,
    ot_src, ot_mid, ot_send,
    gr_src, gr_mid, gr_send, gr_run,
    u_ext, u_t, u_p, o_full, gcat, rs_own, rs_tx, rs_rx,
    local_sem, ag_s, ag_r, rs_s, rs_r, sm_s, sm_r, a2_s, a2_r,
):
    d = lax.axis_index("dp")
    z = lax.axis_index("tensor")

    def mod8(v):
        return lax.rem(v + 16, NZ)

    loads = [
        pltpu.make_async_copy(prompts_hbm.at[0], pr_loc, local_sem.at[0]),
        pltpu.make_async_copy(text_hbm.at[0], text_all.at[z], local_sem.at[1]),
        pltpu.make_async_copy(cot_hbm.at[0], ct_loc, local_sem.at[2]),
        pltpu.make_async_copy(wq_hbm, w_all.at[:, pl.ds(0, WIDTH)], local_sem.at[3]),
        pltpu.make_async_copy(wk_hbm, w_all.at[:, pl.ds(WIDTH, WIDTH)], local_sem.at[4]),
        pltpu.make_async_copy(wv_hbm, w_all.at[:, pl.ds(2 * WIDTH, WIDTH)], local_sem.at[5]),
        pltpu.make_async_copy(cos_hbm, cos_t, local_sem.at[6]),
        pltpu.make_async_copy(sin_hbm, sin_t, local_sem.at[7]),
    ]
    for load in loads:
        load.start()

    barrier = pltpu.get_barrier_semaphore()

    def greet_dp(i, carry):
        pl.semaphore_signal(barrier, inc=1, device_id={"dp": lax.rem(d + i, ND)}, device_id_type=MESH)
        return carry

    def greet_z(i, carry):
        pl.semaphore_signal(barrier, inc=1, device_id={"tensor": lax.rem(z + i, NZ)}, device_id_type=MESH)
        return carry

    lax.fori_loop(1, NZ, greet_z, 0)
    lax.fori_loop(1, ND, greet_dp, 0)

    def remote(src, dst, s_sem, r_sem, where):
        return pltpu.make_async_remote_copy(
            src_ref=src, dst_ref=dst, send_sem=s_sem, recv_sem=r_sem, device_id=where, device_id_type=MESH
        )

    mine_r = lax.div(d * R_PIECES + ND - 1, ND)
    there_r = jnp.logical_and(mine_r < R_PIECES, lax.div(mine_r * ND, R_PIECES) == d)
    PP, CT, OT, GR, SP = range(5)

    def scatter_one(src, mid, which, p, m):
        @pl.when(m != d)
        def _():
            remote(src.at[p], mid.at[d], a2_s.at[which, 0], a2_r.at[which, 0], {"dp": m}).start()

        @pl.when(m == d)
        def _():
            mid[d] = src[p]

    def scatter_rows(src, mid, which):
        def body(i, carry):
            p = lax.rem(d + i, R_PIECES)
            scatter_one(src, mid, which, p, lax.div(p * ND, R_PIECES))
            return carry

        lax.fori_loop(0, R_PIECES, body, 0)

    def scatter_all(src, mid, which):
        def body(i, carry):
            m = lax.rem(d + i, ND)
            remote(src.at[m], mid.at[d], a2_s.at[which, 0], a2_r.at[which, 0], {"dp": m}).start()
            return carry

        lax.fori_loop(1, ND, body, 0)
        mid[d] = src[d]

    def await_bytes(ref, sem, count):
        part = ref.at[pl.ds(0, count)]
        pltpu.make_async_copy(part, part, sem).wait()

    def await_middle(mid, which):
        await_bytes(mid, a2_r.at[which, 0], ND - 1)

    def relay(value, send, dst, which, mine):
        def body(i, carry):
            e = lax.rem(d + i, ND)
            send[e] = value(e)
            remote(send.at[e], dst.at[mine], a2_s.at[which, 1], a2_r.at[which, 1], {"dp": e}).start()
            return carry

        lax.fori_loop(1, ND, body, 0)
        dst[mine] = value(d)

    def await_rows(ref, sem):
        @pl.when(there_r)
        def _():
            await_bytes(ref, sem, R_PIECES - 1)

        @pl.when(jnp.logical_not(there_r))
        def _():
            await_bytes(ref, sem, R_PIECES)

    def send_small(ref, which):
        def body(i, carry):
            remote(ref.at[z], ref.at[z], sm_s.at[which], sm_r.at[which], {"tensor": lax.rem(z + i, NZ)}).start()
            return carry

        lax.fori_loop(1, NZ, body, 0)

    def await_small(ref, sem):
        part = ref.at[pl.ds(0, NZ - 1)]
        pltpu.make_async_copy(part, part, sem).wait()

    SIGN = (1, -1)

    def ring_rows(c, j):
        first, count = SUBS[j]
        return (text_all if j < TEXT_SUB else prm_all).at[c, pl.ds(first, count), :]

    def ring_send(way, k, j):
        rows = ring_rows(mod8(z - SIGN[way] * (k - 1)), j)
        return remote(rows, rows, ag_s.at[way, k - 1, j], ag_r.at[way, k - 1, j], {"tensor": mod8(z + SIGN[way])})

    def ring_recv(way, k, j):
        rows = ring_rows(mod8(z - SIGN[way] * k), j)
        return remote(rows, rows, ag_s.at[way, k - 1, j], ag_r.at[way, k - 1, j], {"tensor": mod8(z + SIGN[way])})

    def ring_step(k, subs):
        for j in subs:
            for way in range(2):
                if k < 4 or j in LAST[way]:
                    ring_recv(way, k, j).wait_recv()
                    if k < 3 or (k == 3 and j in LAST[way]):
                        ring_send(way, k + 1, j).start()

    TEXT_SUBS, PROMPT_SUBS = range(TEXT_SUB), range(TEXT_SUB, len(SUBS))

    def lane_sums(squares, rows):
        return jnp.broadcast_to(jnp.sum(squares, axis=1, keepdims=True), (rows, 128)).T[0:1]

    def total_of(ref):
        total = ref[0]
        for i in range(1, NZ):
            total = total + ref[i]
        return total

    def inverse(squares, rows):
        inv = lax.rsqrt(squares * (1.0 / (NZ * COLS)) + EPS)
        return jnp.broadcast_to(inv, (128, rows)).T

    def project(c):
        for t in range(TILES):
            lanes = slice(128 * t, 128 * t + 128)
            scale = gain[c, :, lanes]
            nb[0:TEXT, lanes] = (text_all[c, :, lanes].astype(F32) * inv_t[...] * scale).astype(BF)
            nb[TEXT:, lanes] = (prm_all[c, :, lanes].astype(F32) * inv_p[...] * scale).astype(BF)
        rows = pl.ds(pl.multiple_of(c * COLS, COLS), COLS)
        for n in range(3):
            wide = slice(WIDTH * n, WIDTH * n + WIDTH)
            acc[:, wide] += dot(nb[...], w_all[rows, wide])

    def project_each(k, count):
        def body(i, carry):
            project(mod8(z + k * (i - 1) if count == 3 else z + k * (2 * i - 1)))
            return carry

        lax.fori_loop(0, count, body, 0)

    loads[0].wait()
    for c in range(TILES):
        for g in range(G_HIGH):
            pp_src[c * G_HIGH + g] = pr_loc[G_ROWS * g : G_ROWS * g + G_ROWS, 128 * c : 128 * c + 128]
    first, second = tail_rows([pr_loc[96:100, 128 * c : 128 * c + 128].astype(F32) for c in range(TILES)])
    pp_src[30] = first.astype(BF)
    pp_src[31] = second.astype(BF)
    total = jnp.zeros((PROMPT, 128), F32)
    for c in range(TILES):
        x = pr_loc[:, 128 * c : 128 * c + 128].astype(F32)
        total = total + x * x
    total = jnp.concatenate([total, jnp.zeros((PROMPT_PAD - PROMPT, 128), F32)], axis=0)
    ssp_all[z] = lane_sums(total, PROMPT_PAD)
    loads[1].wait()
    total = jnp.zeros((TEXT, 128), F32)
    for c in range(TILES):
        x = text_all[z, :, 128 * c : 128 * c + 128].astype(F32)
        total = total + x * x
    sst_all[z] = lane_sums(total, TEXT)
    def look_up(s, carry):
        found, upto = jnp.int32(0), jnp.int32(0)
        for e in range(ND):
            found = jnp.where(slot[e] == s, e, found)
            upto = upto + jnp.where(task_of[e] <= s, 1, 0)
        inverse_slot[s] = found
        last_of[s] = upto - 1
        return carry

    lax.fori_loop(0, ND, look_up, 0)
    pl.semaphore_wait(barrier, ND - 1 + NZ - 1)
    send_small(ssp_all, 1)
    send_small(sst_all, 0)
    for j in TEXT_SUBS:
        for way in range(2):
            ring_send(way, 1, j).start()
    scatter_all(pp_src, pp_mid, PP)
    loads[2].wait()
    for c in range(HEADS):
        lanes = slice(128 * c, 128 * c + 128)
        for g in range(R_HIGH - 1):
            ct_src[c * R_HIGH + g] = ct_loc[R_ROWS * g : R_ROWS * g + R_ROWS, lanes]
        ct_src[c * R_HIGH + 8] = jnp.zeros((R_ROWS, 128), BF)
        ct_src[c * R_HIGH + 8, 0:36] = ct_loc[320:356, lanes]
    prm_all[:, PROMPT_SENT:, :] = jnp.zeros((NZ, PROMPT_PAD - PROMPT_SENT, COLS), BF)
    acc[...] = jnp.zeros_like(acc)
    await_bytes(ssp_all, sm_r.at[1], NZ - 1)
    spt_all[d] = total_of(ssp_all)

    def tell_dp(i, carry):
        m = lax.rem(d + i, ND)
        remote(spt_all.at[d], spt_all.at[d], a2_s.at[SP, 0], a2_r.at[SP, 0], {"dp": m}).start()
        return carry

    lax.fori_loop(1, ND, tell_dp, 0)
    ring_step(1, (0,))
    await_middle(pp_mid, PP)
    relay(lambda e: pp_mid[task_of[e]], pp_send, pp_dst, PP, d)
    ring_step(1, (1, 2))
    await_bytes(sst_all, sm_r.at[0], NZ - 1)
    inv_t[...] = inverse(total_of(sst_all), TEXT)
    ring_step(1, (3,))
    await_bytes(pp_dst, a2_r.at[PP, 1], ND - 1)
    for c in range(TILES):
        lanes = slice(128 * c, 128 * c + 128)
        for g in range(G_HIGH):
            prm_all[z, G_ROWS * g : G_ROWS * g + G_ROWS, lanes] = pp_dst[c * G_HIGH + g]
        end = pp_dst[30 + c // 4].astype(F32)[4 * (c % 4) : 4 * (c % 4) + 4]
        prm_all[z, 96:104, lanes] = jnp.concatenate([end, jnp.zeros((4, 128), F32)], axis=0).astype(BF)
    for j in PROMPT_SUBS:
        for way in range(2):
            ring_send(way, 1, j).start()
    scatter_rows(ct_src, ct_mid, CT)
    ring_step(2, TEXT_SUBS)
    await_bytes(spt_all, a2_r.at[SP, 0], ND - 1)
    inv_p[...] = inverse(spt_all[task_of[d]], PROMPT_PAD)
    ring_step(1, PROMPT_SUBS)
    for load in loads[3:6]:
        load.wait()
    project_each(1, 3)
    ring_step(3, TEXT_SUBS)
    @pl.when(there_r)
    def _():
        await_middle(ct_mid, CT)
        relay(lambda e: ct_mid[slot[e]], ct_send, ct_dst, CT, mine_r)

    ring_step(2, PROMPT_SUBS)
    project_each(2, 2)
    ring_step(4, TEXT_SUBS)
    ring_step(3, PROMPT_SUBS)
    project_each(3, 2)
    length = lengths[d]
    await_rows(ct_dst, a2_r.at[CT, 1])
    for c in range(HEADS):
        for g in range(R_HIGH):
            u_ext[R_ROWS * g : R_ROWS * g + R_ROWS, 128 * c : 128 * c + 128] = ct_dst[c * R_HIGH + g].astype(F32)
    u_ext[R_ROWS * R_HIGH :] = jnp.zeros((ROWS_PAD - R_ROWS * R_HIGH, WIDTH), F32)
    text_row = lax.broadcasted_iota(jnp.int32, (TEXT, 128), 0)
    prompt_row = lax.broadcasted_iota(jnp.int32, (PROMPT_PAD, 128), 0)
    for h in range(HEADS):
        lanes = slice(HD * h, HD * h + HD)
        x = u_ext[:, lanes]
        shifted = pltpu.roll(x, ROWS_PAD - PROMPT, 0)
        u_t[:, lanes] = jnp.where(text_row < length, shifted[0:TEXT], 0.0).astype(BF)
        u_p[:, lanes] = jnp.where(prompt_row < PROMPT, x[0:PROMPT_PAD], 0.0).astype(BF)
    loads[6].wait()
    loads[7].wait()

    ring_step(4, PROMPT_SUBS)
    project(mod8(z + 4))

    score_scale = 1.0 / math.sqrt(HD)
    cos_all, sin_all = cos_t[...], sin_t[...]
    cos_p, sin_p = cos_all[TEXT:], sin_all[TEXT:]
    row_tt = lax.broadcasted_iota(jnp.int32, (TEXT, TEXT), 0)
    col_tt = lax.broadcasted_iota(jnp.int32, (TEXT, TEXT), 1)
    ok_tt = (col_tt <= row_tt) & (col_tt < length)
    ok_tp = lax.broadcasted_iota(jnp.int32, (TEXT, PROMPT_PAD), 1) < PROMPT
    row_pp = lax.broadcasted_iota(jnp.int32, (PROMPT_PAD, PROMPT_PAD), 0)
    col_pp = lax.broadcasted_iota(jnp.int32, (PROMPT_PAD, PROMPT_PAD), 1)
    ok_pp = (col_pp <= row_pp) & (col_pp < PROMPT)
    s_part = jnp.zeros((PROMPT_PAD, HD), F32)
    for h in range(HEADS):
        lanes = slice(HD * h, HD * h + HD)
        pre_q = acc[:, HD * h : HD * h + HD]
        pre_k = acc[:, WIDTH + HD * h : WIDTH + HD * h + HD]
        pre_v = acc[:, 2 * WIDTH + HD * h : 2 * WIDTH + HD * h + HD]
        q = (pre_q * cos_all + pltpu.roll(pre_q, HALF, 1) * sin_all).astype(BF)
        k = (pre_k * cos_all + pltpu.roll(pre_k, HALF, 1) * sin_all).astype(BF)
        v = pre_v.astype(BF)
        qt, qp, kt, kp, vt, vp = q[:TEXT], q[TEXT:], k[:TEXT], k[TEXT:], v[:TEXT], v[TEXT:]
        s_tt = jnp.where(ok_tt, dot_t(qt, kt) * score_scale, -1e30)
        s_tp = jnp.where(ok_tp, dot_t(qt, kp) * score_scale, -1e30)
        s_pp = jnp.where(ok_pp, dot_t(qp, kp) * score_scale, -1e30)
        peak = jnp.maximum(jnp.max(s_tt, axis=1, keepdims=True), jnp.max(s_tp, axis=1, keepdims=True))
        e_tt = jnp.where(ok_tt, jnp.exp(s_tt - peak), 0.0)
        e_tp = jnp.where(ok_tp, jnp.exp(s_tp - peak), 0.0)
        norm = 1.0 / (jnp.sum(e_tt, axis=1, keepdims=True) + jnp.sum(e_tp, axis=1, keepdims=True))
        p_tt, p_tp = e_tt * norm, e_tp * norm
        e_pp = jnp.where(ok_pp, jnp.exp(s_pp - jnp.max(s_pp, axis=1, keepdims=True)), 0.0)
        p_pp = e_pp * (1.0 / jnp.sum(e_pp, axis=1, keepdims=True))
        mixed = dot(p_tt.astype(BF), vt) + dot(p_tp.astype(BF), vp)
        o_full[0:TEXT, lanes] = jnp.where(text_row < length, mixed, 0.0)
        o_full[TEXT:, lanes] = dot(p_pp.astype(BF), vp)
        ut, up = u_t[:, lanes], u_p[:, lanes]
        d_tt, d_tp, d_pp = dot_t(ut, vt), dot_t(ut, vp), dot_t(up, vp)
        delta_t = jnp.sum(p_tt * d_tt, axis=1, keepdims=True) + jnp.sum(p_tp * d_tp, axis=1, keepdims=True)
        g_tp = p_tp * (d_tp - delta_t)
        g_pp = p_pp * (d_pp - jnp.sum(p_pp * d_pp, axis=1, keepdims=True))
        grad_q = dot(g_pp.astype(BF), kp) * score_scale
        grad_k = (dot(g_tp.T.astype(BF), qt) + dot(g_pp.T.astype(BF), qp)) * score_scale
        grad_v = (dot(p_tp.T.astype(BF), ut) + dot(p_pp.T.astype(BF), up)).astype(BF)
        grad_q = (grad_q * cos_p - pltpu.roll(grad_q, HALF, 1) * sin_p).astype(BF)
        grad_k = (grad_k * cos_p - pltpu.roll(grad_k, HALF, 1) * sin_p).astype(BF)
        gcat[:, HD * h : HD * h + HD] = grad_q
        gcat[:, WIDTH + HD * h : WIDTH + HD * h + HD] = grad_k
        gcat[:, 2 * WIDTH + HD * h : 2 * WIDTH + HD * h + HD] = grad_v
        s_part = s_part + grad_q.astype(F32) * pre_q[TEXT:] + grad_k.astype(F32) * pre_k[TEXT:]
        s_part = s_part + grad_v.astype(F32) * pre_v[TEXT:]

    def grad_block(j):
        rows = pl.ds(pl.multiple_of(j * COLS, COLS), COLS)
        return dot_t(gcat[0:PROMPT_SENT], w_all[rows, :])

    def rs_copy(way, step, t):
        return remote(
            rs_tx.at[way, step, t], rs_rx.at[way, step, t], rs_s.at[way, step, t], rs_r.at[way, step, t],
            {"tensor": mod8(z + SIGN[way])},
        )

    def rs_put(way, step, t, value):
        rs_tx[way, step, t] = value.astype(BF)
        rs_copy(way, step, t).start()

    block = grad_block(mod8(z + 4))
    for way in range(2):
        for t in RS_LAST[way]:
            rs_put(way, 0, t, block[:, 128 * t : 128 * t + 128])
    blocks = (grad_block(mod8(z + 3)), grad_block(mod8(z - 3)))
    for way in range(2):
        for t in RS_LAST[1 - way]:
            rs_put(way, 1, t, blocks[way][:, 128 * t : 128 * t + 128])
    for way in range(2):
        for t in RS_LAST[way]:
            rs_own[way, t] = blocks[way][:, 128 * t : 128 * t + 128]
    sx_all[z] = lane_sums(s_part, PROMPT_PAD)
    send_small(sx_all, 2)

    for h in range(HEADS):
        lanes = slice(HD * h, HD * h + HD)
        x = o_full[:, lanes]
        head_row = lax.broadcasted_iota(jnp.int32, (ROWS_PAD, 128), 0)
        outer = jnp.where(head_row < PROMPT, jnp.concatenate([x[TEXT:], x[:TEXT]], axis=0), pltpu.roll(x, PROMPT, 0))
        outer = outer.astype(BF)
        for g in range(R_HIGH):
            ot_src[h * R_HIGH + g] = outer[R_ROWS * g : R_ROWS * g + R_ROWS]
    scatter_rows(ot_src, ot_mid, OT)

    for t in (0, 1, 2):
        for way in range(2):
            if t < len(RS_LAST[way]):
                tile = RS_LAST[way][t]
                rs_copy(way, 0, tile).wait_recv()
                rs_put(way, 1, tile, rs_own[way, tile] + rs_rx[way, 0, tile].astype(F32))
    for step in (2, 3):
        blocks = (grad_block(mod8(z + 4 - step)), grad_block(mod8(z - 4 + step)))
        for i in range(TILES):
            for way in range(2):
                t = RS_ORDER[way][i]
                rs_copy(way, step - 1, t).wait_recv()
                value = blocks[way][:, 128 * t : 128 * t + 128] + rs_rx[way, step - 1, t].astype(F32)
                rs_put(way, step, t, value)
        if step == 2:

            @pl.when(there_r)
            def _():
                await_middle(ot_mid, OT)
                relay(lambda s: ot_mid[inverse_slot[s]], ot_send, ot_dst, OT, mine_r)

    own = grad_block(z)
    await_bytes(sx_all, sm_r.at[2], NZ - 1)
    s_col[...] = jnp.broadcast_to(total_of(sx_all) * (1.0 / (NZ * COLS)), (128, PROMPT_PAD)).T
    inv = inv_p[0:PROMPT_SENT]
    second = inv * inv * s_col[0:PROMPT_SENT]
    ends = []
    for t in range(TILES):
        lanes = slice(128 * t, 128 * t + 128)
        value = own[:, lanes]
        for way in range(2):
            rs_copy(way, 3, t).wait_recv()
            value = value + rs_rx[way, 3, t].astype(F32)
        value = inv * (value * gain[z, :, lanes]) - prm_all[z, 0:PROMPT_SENT, lanes].astype(F32) * second
        low = value.astype(BF)
        for g in range(G_HIGH):
            p = t * G_HIGH + g
            gr_src[p] = low[G_ROWS * g : G_ROWS * g + G_ROWS]
            scatter_one(gr_src, gr_mid, GR, p, p)
        ends.append(value[96:100])
    first, second = tail_rows(ends)
    for p, value in ((30, first), (31, second)):
        gr_src[p] = value.astype(BF)
        scatter_one(gr_src, gr_mid, GR, p, p)
    await_middle(gr_mid, GR)
    before = jnp.zeros((G_ROWS, 128), F32)
    for e in range(ND):
        now = gr_mid[e].astype(F32)
        if e > 0:
            now = now + jnp.where(task_of[e] == task_of[e - 1], before, 0.0)
        gr_run[e] = now
        before = now

    def task_sum(t):
        at = jnp.maximum(last_of[t], 0)
        return jnp.where(task_of[at] == t, gr_run[at], 0.0).astype(BF)

    relay(task_sum, gr_send, gr_dst, GR, d)
    await_rows(ot_dst, a2_r.at[OT, 1])
    await_bytes(gr_dst, a2_r.at[GR, 1], ND - 1)
    await_bytes(spt_all, a2_s.at[SP, 0], ND - 1)
    await_bytes(pp_src, a2_s.at[PP, 0], ND - 1)
    await_bytes(pp_send, a2_s.at[PP, 1], ND - 1)
    await_bytes(gr_src, a2_s.at[GR, 0], ND - 1)
    await_bytes(gr_send, a2_s.at[GR, 1], ND - 1)
    await_rows(ct_src, a2_s.at[CT, 0])
    await_rows(ot_src, a2_s.at[OT, 0])

    @pl.when(there_r)
    def _():
        await_bytes(ct_send, a2_s.at[CT, 1], ND - 1)
        await_bytes(ot_send, a2_s.at[OT, 1], ND - 1)

    for which, ref in enumerate((sst_all, ssp_all, sx_all)):
        await_bytes(ref, sm_s.at[which], NZ - 1)
    for way in range(2):
        for j in range(len(SUBS)):
            for k in range(1, 5):
                if k < 4 or j in LAST[way]:
                    ring_send(way, k, j).wait_send()
        for step in range(4):
            for t in range(TILES):
                if step > 0 or t in RS_LAST[way]:
                    rs_copy(way, step, t).wait_send()


def assemble(ot_ref, gr_ref, out_ref, pg_ref):
    for c in range(HEADS):
        lanes = slice(128 * c, 128 * c + 128)
        for g in range(R_HIGH - 1):
            out_ref[0, R_ROWS * g : R_ROWS * g + R_ROWS, lanes] = ot_ref[c * R_HIGH + g]
        out_ref[0, 320:356, lanes] = ot_ref[c * R_HIGH + 8, 0:36]
    for c in range(TILES):
        lanes = slice(128 * c, 128 * c + 128)
        for g in range(G_HIGH):
            pg_ref[G_ROWS * g : G_ROWS * g + G_ROWS, 0, lanes] = gr_ref[c * G_HIGH + g].astype(F32)
        pg_ref[96:100, 0, lanes] = gr_ref[30 + c // 4].astype(F32)[4 * (c % 4) : 4 * (c % 4) + 4]


def on_device(text, prompts, gain, w_query, w_key, w_value, cotangent, task_of, lengths, slot):
    cosine, sine = rope_constants()
    vmem, dma, smem = pltpu.VMEM, pltpu.SemaphoreType.DMA, pltpu.SMEM
    anywhere = pl.BlockSpec(memory_space=pl.ANY)
    whole = pl.BlockSpec(memory_space=pltpu.VMEM)
    scalars = pl.BlockSpec(memory_space=pltpu.SMEM)
    g_piece, r_piece = (G_ROWS, 128), (R_ROWS, 128)
    out_pieces, grad_pieces = pl.pallas_call(
        kernel,
        out_shape=(
            pltpu.VMEM((R_PIECES, *r_piece), BF),
            pltpu.VMEM((ND, *g_piece), BF),
        ),
        in_specs=[scalars] * 3 + [anywhere, anywhere, whole] + [anywhere] * 6,
        out_specs=(whole, whole),
        scratch_shapes=[
            smem((ND,), jnp.int32), smem((ND,), jnp.int32),
            vmem((NZ, TEXT, COLS), BF), vmem((NZ, PROMPT_PAD, COLS), BF), vmem((PROMPT, COLS), BF),
            vmem((ROWS, WIDTH), BF), vmem((NZ * COLS, ALL), BF),
            vmem((ROWS_PAD, HD), F32), vmem((ROWS_PAD, HD), F32),
            vmem((ROWS_PAD, ALL), F32), vmem((ROWS_PAD, COLS), BF),
            vmem((TEXT, 128), F32), vmem((PROMPT_PAD, 128), F32), vmem((PROMPT_PAD, 128), F32),
            vmem((NZ, 1, TEXT), F32), vmem((NZ, 1, PROMPT_PAD), F32), vmem((ND, 1, PROMPT_PAD), F32),
            vmem((NZ, 1, PROMPT_PAD), F32),
            vmem((ND, *g_piece), BF), vmem((ND, *g_piece), BF), vmem((ND, *g_piece), BF), vmem((ND, *g_piece), BF),
            vmem((R_PIECES, *r_piece), BF), vmem((ND, *r_piece), BF), vmem((ND, *r_piece), BF), vmem((R_PIECES, *r_piece), BF),
            vmem((R_PIECES, *r_piece), BF), vmem((ND, *r_piece), BF), vmem((ND, *r_piece), BF),
            vmem((ND, *g_piece), BF), vmem((ND, *g_piece), BF), vmem((ND, *g_piece), BF), vmem((ND, *g_piece), F32),
            vmem((ROWS_PAD, WIDTH), F32), vmem((TEXT, WIDTH), BF), vmem((PROMPT_PAD, WIDTH), BF),
            vmem((ROWS_PAD, WIDTH), F32), vmem((PROMPT_PAD, ALL), BF),
            vmem((2, TILES, PROMPT_SENT, 128), F32),
            vmem((2, 4, TILES, PROMPT_SENT, 128), BF), vmem((2, 4, TILES, PROMPT_SENT, 128), BF),
            dma((8,)), dma((2, 4, len(SUBS))), dma((2, 4, len(SUBS))), dma((2, 4, TILES)), dma((2, 4, TILES)),
            dma((3,)), dma((3,)), dma((5, 2)), dma((5, 2)),
        ],
        compiler_params=pltpu.CompilerParams(
            collective_id=0, has_side_effects=True, vmem_limit_bytes=56 * 1024 * 1024
        ),
    )(
        task_of, lengths, slot, text, prompts, gain.reshape(NZ, 1, COLS), w_query, w_key, w_value, cotangent,
        jnp.asarray(cosine), jnp.asarray(sine),
    )
    attn_out, prompt_grad = pl.pallas_call(
        assemble,
        out_shape=(
            jax.ShapeDtypeStruct((1, ROWS, WIDTH), BF),
            jax.ShapeDtypeStruct((PROMPT, 1, COLS), F32),
        ),
        in_specs=[whole, whole],
        out_specs=(whole, whole),
    )(*(pltpu.with_memory_space_constraint(x, pltpu.VMEM) for x in (out_pieces, grad_pieces)))
    return attn_out, prompt_grad.reshape(1, PROMPT, COLS)


def solution(mesh):
    in_specs = (
        P("dp", None, "tensor"),
        P("dp", None, "tensor"),
        P(),
        P(None, "tensor"),
        P(None, "tensor"),
        P(None, "tensor"),
        P("dp", None, "tensor"),
        P(),
        P(),
        P(),
    )
    out_specs = (P("dp", None, "tensor"), P("dp", None, "tensor"))
    return jax.shard_map(on_device, mesh=mesh, in_specs=in_specs, out_specs=out_specs, check_vma=False)
```

time: 94.9 us -> 83.6 us (0.88)
  local copies, waits for them, and re-layouts: 4.94 us -> 0 us
  Pallas kernels: 86.7 us -> 82.8 us
  other arithmetic: 2.43 us -> 0 us
    pallas_call x1 -> x2, Pallas kernels: 86.7 us -> 82.8 us  [the longest x1 81.9 us: on_device(): pl.pallas_call(kernel, out_shape=(pltpu.VMEM((R_PIECES, *r_piece), BF), p...]
    pallas_call x1 -> x0, local copies, waits for them, and re-layouts: 1.91 us -> none  [on_device(): pl.pallas_call(kernel, out_shape=(jax.ShapeDtypeStruct((1, ROWS, WIDTH),...]
    unnamed x1 -> x0, local copies, waits for them, and re-layouts: 1.69 us -> none
    reduce_sum x2 -> x0, other arithmetic: 1.54 us -> none  [the longest x1 0.77 us: on_device(): jnp.sum(jnp.where(slot[None, :] == order[:, None], order[None, :], 0), ax...]
    another operation x1 -> x0, local copies, waits for them, and re-layouts: 1.34 us -> none  [on_device(): jnp.stack([task_of, slot, inverse, jnp.maximum(upto - 1, 0), here, same,...]
where the time goes in v2:
time: 83.6 us; the launch traced here: 83.4 us
  Pallas kernels  82.8 us (99%)
    pallas_call x1, Pallas kernels, on_device(): pl.pallas_call(kernel, out_shape=(pltpu.VMEM((R_PIECES, *r_piece), BF), p...  81.9 us

profile of v2, /device:TPU:1, one launch (start us, length us, event | category | flops | bytes accessed | tf_op | source)
XLA Modules:
  0.0 83.4 jit_solution(3375390122336546306)
XLA Ops:
  0.6 81.9 %shard_map.131 = (bf16[27,40,128]{2,1,0:T(8,128)(2,1)S(1)}, bf16[32,16,128]{2,1,0:T(8,128)(2,1)S(1)}) custom-call(s32[32]{0:T(128)} %task_of.1, s32[32]{0:T(128)} %lengths.1, s32[32]{0:T(128)} %slot.1, bf16[1,256,640]{2,1,0:T(8,128)(2,1)} %text_hbm.1, bf16[1,100,640]{2,1,0:T(8,128)(2,1)} %prompts_hbm.1, f32[8,1,640]{2,1,0:T(1,128)} %bitcast.2, ...), custom_call_target="tpu_custom_call" | custom-call | tf_op jit(solution)/shard_map/pallas_call | solution.py:540
  82.5 0.9 %shard_map.132 = (bf16[1,356,384]{2,1,0:T(8,128)(2,1)}, f32[100,1,640]{2,1,0:T(1,128)}) custom-call(bf16[27,40,128]{2,1,0:T(8,128)(2,1)S(1)} %get-tuple-element.6.ot_ref, bf16[32,16,128]{2,1,0:T(8,128)(2,1)S(1)} %get-tuple-element.7.gr_ref), custom_call_target="tpu_custom_call" | custom-call | tf_op jit(solution)/shard_map/pallas_call | solution.py:575

commit v3 on v2

--- a/solution.py
+++ b/solution.py
@@ -36,13 +36,16 @@
 TEXT_SUB = 4
 SUBS = ((0, 64), (64, 64), (128, 64), (192, 64), (0, 56), (56, 48))
 LAST = ((0, 1, 4), (2, 3, 5))
+LATE = (1, 3)
+TEXT_ORDER = ((0, 2), (1, 3), (2, 0), (3, 1))
+PROMPT_ORDER = ((4, 5), (5, 4))
 RS_LAST = ((0, 1, 2), (3, 4))
 RS_ORDER = ((3, 4, 0, 1, 2), (0, 1, 2, 3, 4))
 
 
 def rope_constants():
     frequency = (np.float32(10000.0) ** (-np.arange(HALF, dtype=np.float32) / np.float32(HALF))).astype(np.float32)
-    position = np.concatenate([np.arange(TEXT) + PROMPT, np.arange(PROMPT_PAD)]).astype(np.float32)
+    position = np.concatenate([np.arange(PROMPT_PAD), np.arange(TEXT) + PROMPT]).astype(np.float32)
     angle = (position[:, None] * frequency[None, :]).astype(np.float32)
     cosine = np.cos(angle.astype(np.float64)).astype(np.float32)
     sine = np.sin(angle.astype(np.float64)).astype(np.float32)
@@ -63,16 +66,16 @@
 
 
 def kernel(
-    task_of, lengths, slot, text_hbm, prompts_hbm, gain, wq_hbm, wk_hbm, wv_hbm, cot_hbm, cos_hbm, sin_hbm,
+    task_hbm, lengths_hbm, slot_hbm, text_hbm, prompts_hbm, gain_hbm, wq_hbm, wk_hbm, wv_hbm, cot_hbm, cos_hbm, sin_hbm,
     ot_dst, gr_dst,
-    inverse_slot, last_of,
+    task_of, lengths, slot, inverse_slot, last_of, gain,
     text_all, prm_all, pr_loc, ct_loc, w_all, cos_t, sin_t, acc, nb, inv_t, inv_p, s_col,
     sst_all, ssp_all, spt_all, sx_all,
     pp_src, pp_mid, pp_send, pp_dst,
     ct_src, ct_mid, ct_send, ct_dst,
     ot_src, ot_mid, ot_send,
     gr_src, gr_mid, gr_send, gr_run,
-    u_ext, u_t, u_p, o_full, gcat, rs_own, rs_tx, rs_rx,
+    u_ext, u_all, o_full, gcat, rs_own, rs_tx, rs_rx,
     local_sem, ag_s, ag_r, rs_s, rs_r, sm_s, sm_r, a2_s, a2_r,
 ):
     d = lax.axis_index("dp")
@@ -90,10 +93,11 @@
         pltpu.make_async_copy(wv_hbm, w_all.at[:, pl.ds(2 * WIDTH, WIDTH)], local_sem.at[5]),
         pltpu.make_async_copy(cos_hbm, cos_t, local_sem.at[6]),
         pltpu.make_async_copy(sin_hbm, sin_t, local_sem.at[7]),
+        pltpu.make_async_copy(gain_hbm, gain, local_sem.at[8]),
+        pltpu.make_async_copy(task_hbm, task_of, local_sem.at[9]),
+        pltpu.make_async_copy(lengths_hbm, lengths, local_sem.at[10]),
+        pltpu.make_async_copy(slot_hbm, slot, local_sem.at[11]),
     ]
-    for load in loads:
-        load.start()
-
     barrier = pltpu.get_barrier_semaphore()
 
     def greet_dp(i, carry):
@@ -106,6 +110,8 @@
 
     lax.fori_loop(1, NZ, greet_z, 0)
     lax.fori_loop(1, ND, greet_dp, 0)
+    for load in loads:
+        load.start()
 
     def remote(src, dst, s_sem, r_sem, where):
         return pltpu.make_async_remote_copy(
@@ -193,15 +199,18 @@
         rows = ring_rows(mod8(z - SIGN[way] * k), j)
         return remote(rows, rows, ag_s.at[way, k - 1, j], ag_r.at[way, k - 1, j], {"tensor": mod8(z + SIGN[way])})
 
-    def ring_step(k, subs):
-        for j in subs:
-            for way in range(2):
+    def ring_step(k, pairs):
+        for pair in pairs:
+            for way, j in enumerate(pair):
                 if k < 4 or j in LAST[way]:
                     ring_recv(way, k, j).wait_recv()
-                    if k < 3 or (k == 3 and j in LAST[way]):
+                    if k < 3 or (k == 3 and j in LAST[way] and j not in LATE):
                         ring_send(way, k + 1, j).start()
 
-    TEXT_SUBS, PROMPT_SUBS = range(TEXT_SUB), range(TEXT_SUB, len(SUBS))
+    def ring_begin(pairs):
+        for pair in pairs:
+            for way, j in enumerate(pair):
+                ring_send(way, 1, j).start()
 
     def lane_sums(squares, rows):
         return jnp.broadcast_to(jnp.sum(squares, axis=1, keepdims=True), (rows, 128)).T[0:1]
@@ -216,16 +225,26 @@
         inv = lax.rsqrt(squares * (1.0 / (NZ * COLS)) + EPS)
         return jnp.broadcast_to(inv, (128, rows)).T
 
-    def project(c):
+    def normed_text(c):
         for t in range(TILES):
             lanes = slice(128 * t, 128 * t + 128)
-            scale = gain[c, :, lanes]
-            nb[0:TEXT, lanes] = (text_all[c, :, lanes].astype(F32) * inv_t[...] * scale).astype(BF)
-            nb[TEXT:, lanes] = (prm_all[c, :, lanes].astype(F32) * inv_p[...] * scale).astype(BF)
+            nb[PROMPT_PAD:, lanes] = (text_all[c, :, lanes].astype(F32) * inv_t[...] * gain[c, :, lanes]).astype(BF)
+
+    def normed_prompts(c):
+        for t in range(TILES):
+            lanes = slice(128 * t, 128 * t + 128)
+            nb[0:PROMPT_PAD, lanes] = (prm_all[c, :, lanes].astype(F32) * inv_p[...] * gain[c, :, lanes]).astype(BF)
+
+    def multiply(c):
         rows = pl.ds(pl.multiple_of(c * COLS, COLS), COLS)
         for n in range(3):
             wide = slice(WIDTH * n, WIDTH * n + WIDTH)
             acc[:, wide] += dot(nb[...], w_all[rows, wide])
+
+    def project(c):
+        normed_text(c)
+        normed_prompts(c)
+        multiply(c)
 
     def project_each(k, count):
         def body(i, carry):
@@ -253,22 +272,10 @@
         x = text_all[z, :, 128 * c : 128 * c + 128].astype(F32)
         total = total + x * x
     sst_all[z] = lane_sums(total, TEXT)
-    def look_up(s, carry):
-        found, upto = jnp.int32(0), jnp.int32(0)
-        for e in range(ND):
-            found = jnp.where(slot[e] == s, e, found)
-            upto = upto + jnp.where(task_of[e] <= s, 1, 0)
-        inverse_slot[s] = found
-        last_of[s] = upto - 1
-        return carry
-
-    lax.fori_loop(0, ND, look_up, 0)
     pl.semaphore_wait(barrier, ND - 1 + NZ - 1)
     send_small(ssp_all, 1)
     send_small(sst_all, 0)
-    for j in TEXT_SUBS:
-        for way in range(2):
-            ring_send(way, 1, j).start()
+    ring_begin(TEXT_ORDER)
     scatter_all(pp_src, pp_mid, PP)
     loads[2].wait()
     for c in range(HEADS):
@@ -279,6 +286,18 @@
         ct_src[c * R_HIGH + 8, 0:36] = ct_loc[320:356, lanes]
     prm_all[:, PROMPT_SENT:, :] = jnp.zeros((NZ, PROMPT_PAD - PROMPT_SENT, COLS), BF)
     acc[...] = jnp.zeros_like(acc)
+    for load in loads[9:]:
+        load.wait()
+    def look_up(s, carry):
+        found, upto = jnp.int32(0), jnp.int32(0)
+        for e in range(ND):
+            found = jnp.where(slot[e] == s, e, found)
+            upto = upto + jnp.where(task_of[e] <= s, 1, 0)
+        inverse_slot[s] = found
+        last_of[s] = upto - 1
+        return carry
+
+    lax.fori_loop(0, ND, look_up, 0)
     await_bytes(ssp_all, sm_r.at[1], NZ - 1)
     spt_all[d] = total_of(ssp_all)
 
@@ -288,13 +307,13 @@
         return carry
 
     lax.fori_loop(1, ND, tell_dp, 0)
-    ring_step(1, (0,))
+    ring_step(1, TEXT_ORDER[:1])
     await_middle(pp_mid, PP)
     relay(lambda e: pp_mid[task_of[e]], pp_send, pp_dst, PP, d)
-    ring_step(1, (1, 2))
+    ring_step(1, TEXT_ORDER[1:3])
     await_bytes(sst_all, sm_r.at[0], NZ - 1)
     inv_t[...] = inverse(total_of(sst_all), TEXT)
-    ring_step(1, (3,))
+    ring_step(1, TEXT_ORDER[3:])
     await_bytes(pp_dst, a2_r.at[PP, 1], ND - 1)
     for c in range(TILES):
         lanes = slice(128 * c, 128 * c + 128)
@@ -302,27 +321,26 @@
             prm_all[z, G_ROWS * g : G_ROWS * g + G_ROWS, lanes] = pp_dst[c * G_HIGH + g]
         end = pp_dst[30 + c // 4].astype(F32)[4 * (c % 4) : 4 * (c % 4) + 4]
         prm_all[z, 96:104, lanes] = jnp.concatenate([end, jnp.zeros((4, 128), F32)], axis=0).astype(BF)
-    for j in PROMPT_SUBS:
-        for way in range(2):
-            ring_send(way, 1, j).start()
+    ring_begin(PROMPT_ORDER)
     scatter_rows(ct_src, ct_mid, CT)
-    ring_step(2, TEXT_SUBS)
+    ring_step(2, TEXT_ORDER)
     await_bytes(spt_all, a2_r.at[SP, 0], ND - 1)
     inv_p[...] = inverse(spt_all[task_of[d]], PROMPT_PAD)
-    ring_step(1, PROMPT_SUBS)
-    for load in loads[3:6]:
+    ring_step(1, PROMPT_ORDER)
+    for load in loads[3:6] + loads[8:9]:
         load.wait()
     project_each(1, 3)
-    ring_step(3, TEXT_SUBS)
+    ring_step(3, TEXT_ORDER)
     @pl.when(there_r)
     def _():
         await_middle(ct_mid, CT)
         relay(lambda e: ct_mid[slot[e]], ct_send, ct_dst, CT, mine_r)
 
-    ring_step(2, PROMPT_SUBS)
+    ring_step(2, PROMPT_ORDER)
+    for way in range(2):
+        ring_send(way, 4, LATE[way]).start()
     project_each(2, 2)
-    ring_step(4, TEXT_SUBS)
-    ring_step(3, PROMPT_SUBS)
+    ring_step(3, PROMPT_ORDER)
     project_each(3, 2)
     length = lengths[d]
     await_rows(ct_dst, a2_r.at[CT, 1])
@@ -330,68 +348,74 @@
         for g in range(R_HIGH):
             u_ext[R_ROWS * g : R_ROWS * g + R_ROWS, 128 * c : 128 * c + 128] = ct_dst[c * R_HIGH + g].astype(F32)
     u_ext[R_ROWS * R_HIGH :] = jnp.zeros((ROWS_PAD - R_ROWS * R_HIGH, WIDTH), F32)
-    text_row = lax.broadcasted_iota(jnp.int32, (TEXT, 128), 0)
-    prompt_row = lax.broadcasted_iota(jnp.int32, (PROMPT_PAD, 128), 0)
+    row = lax.broadcasted_iota(jnp.int32, (ROWS_PAD, HD), 0)
+    live = (row < PROMPT) | ((row >= PROMPT_PAD) & (row < length + PROMPT_PAD))
     for h in range(HEADS):
         lanes = slice(HD * h, HD * h + HD)
         x = u_ext[:, lanes]
-        shifted = pltpu.roll(x, ROWS_PAD - PROMPT, 0)
-        u_t[:, lanes] = jnp.where(text_row < length, shifted[0:TEXT], 0.0).astype(BF)
-        u_p[:, lanes] = jnp.where(prompt_row < PROMPT, x[0:PROMPT_PAD], 0.0).astype(BF)
+        x = jnp.where(row < PROMPT_PAD, x, pltpu.roll(x, PROMPT_PAD - PROMPT, 0))
+        u_all[:, lanes] = jnp.where(live, x, 0.0).astype(BF)
     loads[6].wait()
     loads[7].wait()
 
-    ring_step(4, PROMPT_SUBS)
-    project(mod8(z + 4))
+    ring_step(4, TEXT_ORDER)
+    normed_text(mod8(z + 4))
+    ring_step(4, PROMPT_ORDER)
+    normed_prompts(mod8(z + 4))
+    multiply(mod8(z + 4))
 
     score_scale = 1.0 / math.sqrt(HD)
     cos_all, sin_all = cos_t[...], sin_t[...]
-    cos_p, sin_p = cos_all[TEXT:], sin_all[TEXT:]
-    row_tt = lax.broadcasted_iota(jnp.int32, (TEXT, TEXT), 0)
-    col_tt = lax.broadcasted_iota(jnp.int32, (TEXT, TEXT), 1)
-    ok_tt = (col_tt <= row_tt) & (col_tt < length)
-    ok_tp = lax.broadcasted_iota(jnp.int32, (TEXT, PROMPT_PAD), 1) < PROMPT
-    row_pp = lax.broadcasted_iota(jnp.int32, (PROMPT_PAD, PROMPT_PAD), 0)
-    col_pp = lax.broadcasted_iota(jnp.int32, (PROMPT_PAD, PROMPT_PAD), 1)
-    ok_pp = (col_pp <= row_pp) & (col_pp < PROMPT)
+    cos_p, sin_p = cos_all[:PROMPT_PAD], sin_all[:PROMPT_PAD]
+    block_rows = [slice(128 * b, 128 * b + 128) for b in range(3)]
+    allowed = []
+    for b in range(3):
+        shape = (128, 128 * b + 128)
+        r = lax.broadcasted_iota(jnp.int32, shape, 0) + 128 * b
+        c = lax.broadcasted_iota(jnp.int32, shape, 1)
+        allowed.append((c <= r) & ((c < PROMPT) | ((c >= PROMPT_PAD) & (c < length + PROMPT_PAD))))
+    at_q = [slice(HD * h, HD * h + HD) for h in range(HEADS)]
+    at_k = [slice(WIDTH + HD * h, WIDTH + HD * h + HD) for h in range(HEADS)]
+    at_v = [slice(2 * WIDTH + HD * h, 2 * WIDTH + HD * h + HD) for h in range(HEADS)]
+    every = [(h, b) for h in range(HEADS) for b in range(3)]
+
+    def turned(pre):
+        return (pre * cos_all + pltpu.roll(pre, HALF, 1) * sin_all).astype(BF)
+
+    def keys(b):
+        return slice(0, 128 * b + 128)
+
+    q = [turned(acc[:, at_q[h]]) for h in range(HEADS)]
+    k = [turned(acc[:, at_k[h]]) for h in range(HEADS)]
+    v = [acc[:, at_v[h]].astype(BF) for h in range(HEADS)]
+    u = [u_all[:, at_q[h]] for h in range(HEADS)]
+    scores = {
+        (h, b): jnp.where(allowed[b], dot_t(q[h][block_rows[b]], k[h][keys(b)]) * score_scale, -1e30) for h, b in every
+    }
+    grad_prob = {(h, b): dot_t(u[h][block_rows[b]], v[h][keys(b)]) for h, b in every}
+    peak = {at: jnp.max(scores[at], axis=1, keepdims=True) for at in every}
+    weights = {at: jnp.exp(scores[at] - peak[at]) for at in every}
+    norm = {at: 1.0 / jnp.sum(weights[at], axis=1, keepdims=True) for at in every}
+    prob = {at: weights[at] * norm[at] for at in every}
+    delta = {at: jnp.sum(prob[at] * grad_prob[at], axis=1, keepdims=True) for at in every}
+    grads = {
+        at: prob[at][:, :PROMPT_PAD] * (grad_prob[at][:, :PROMPT_PAD] - delta[at]) for at in every
+    }
+    for h, b in every:
+        mixed = dot(prob[h, b].astype(BF), v[h][keys(b)])
+        o_full[block_rows[b], at_q[h]] = mixed if b == 0 else jnp.where(live[block_rows[b]], mixed, 0.0)
+    grad_t = [jnp.concatenate([grads[h, b].T for b in range(3)], axis=1).astype(BF) for h in range(HEADS)]
+    prob_t = [jnp.concatenate([prob[h, b][:, :PROMPT_PAD].T for b in range(3)], axis=1).astype(BF) for h in range(HEADS)]
+    grad_q = [dot(grads[h, 0].astype(BF), k[h][:PROMPT_PAD]) * score_scale for h in range(HEADS)]
+    grad_k = [dot(grad_t[h], q[h]) * score_scale for h in range(HEADS)]
+    grad_v = [dot(prob_t[h], u[h]).astype(BF) for h in range(HEADS)]
+    grad_q = [(g * cos_p - pltpu.roll(g, HALF, 1) * sin_p).astype(BF) for g in grad_q]
+    grad_k = [(g * cos_p - pltpu.roll(g, HALF, 1) * sin_p).astype(BF) for g in grad_k]
     s_part = jnp.zeros((PROMPT_PAD, HD), F32)
     for h in range(HEADS):
-        lanes = slice(HD * h, HD * h + HD)
-        pre_q = acc[:, HD * h : HD * h + HD]
-        pre_k = acc[:, WIDTH + HD * h : WIDTH + HD * h + HD]
-        pre_v = acc[:, 2 * WIDTH + HD * h : 2 * WIDTH + HD * h + HD]
-        q = (pre_q * cos_all + pltpu.roll(pre_q, HALF, 1) * sin_all).astype(BF)
-        k = (pre_k * cos_all + pltpu.roll(pre_k, HALF, 1) * sin_all).astype(BF)
-        v = pre_v.astype(BF)
-        qt, qp, kt, kp, vt, vp = q[:TEXT], q[TEXT:], k[:TEXT], k[TEXT:], v[:TEXT], v[TEXT:]
-        s_tt = jnp.where(ok_tt, dot_t(qt, kt) * score_scale, -1e30)
-        s_tp = jnp.where(ok_tp, dot_t(qt, kp) * score_scale, -1e30)
-        s_pp = jnp.where(ok_pp, dot_t(qp, kp) * score_scale, -1e30)
-        peak = jnp.maximum(jnp.max(s_tt, axis=1, keepdims=True), jnp.max(s_tp, axis=1, keepdims=True))
-        e_tt = jnp.where(ok_tt, jnp.exp(s_tt - peak), 0.0)
-        e_tp = jnp.where(ok_tp, jnp.exp(s_tp - peak), 0.0)
-        norm = 1.0 / (jnp.sum(e_tt, axis=1, keepdims=True) + jnp.sum(e_tp, axis=1, keepdims=True))
-        p_tt, p_tp = e_tt * norm, e_tp * norm
-        e_pp = jnp.where(ok_pp, jnp.exp(s_pp - jnp.max(s_pp, axis=1, keepdims=True)), 0.0)
-        p_pp = e_pp * (1.0 / jnp.sum(e_pp, axis=1, keepdims=True))
-        mixed = dot(p_tt.astype(BF), vt) + dot(p_tp.astype(BF), vp)
-        o_full[0:TEXT, lanes] = jnp.where(text_row < length, mixed, 0.0)
-        o_full[TEXT:, lanes] = dot(p_pp.astype(BF), vp)
-        ut, up = u_t[:, lanes], u_p[:, lanes]
-        d_tt, d_tp, d_pp = dot_t(ut, vt), dot_t(ut, vp), dot_t(up, vp)
-        delta_t = jnp.sum(p_tt * d_tt, axis=1, keepdims=True) + jnp.sum(p_tp * d_tp, axis=1, keepdims=True)
-        g_tp = p_tp * (d_tp - delta_t)
-        g_pp = p_pp * (d_pp - jnp.sum(p_pp * d_pp, axis=1, keepdims=True))
-        grad_q = dot(g_pp.astype(BF), kp) * score_scale
-        grad_k = (dot(g_tp.T.astype(BF), qt) + dot(g_pp.T.astype(BF), qp)) * score_scale
-        grad_v = (dot(p_tp.T.astype(BF), ut) + dot(p_pp.T.astype(BF), up)).astype(BF)
-        grad_q = (grad_q * cos_p - pltpu.roll(grad_q, HALF, 1) * sin_p).astype(BF)
-        grad_k = (grad_k * cos_p - pltpu.roll(grad_k, HALF, 1) * sin_p).astype(BF)
-        gcat[:, HD * h : HD * h + HD] = grad_q
-        gcat[:, WIDTH + HD * h : WIDTH + HD * h + HD] = grad_k
-        gcat[:, 2 * WIDTH + HD * h : 2 * WIDTH + HD * h + HD] = grad_v
-        s_part = s_part + grad_q.astype(F32) * pre_q[TEXT:] + grad_k.astype(F32) * pre_k[TEXT:]
-        s_part = s_part + grad_v.astype(F32) * pre_v[TEXT:]
+        for at, grad in ((at_q[h], grad_q[h]), (at_k[h], grad_k[h]), (at_v[h], grad_v[h])):
+            gcat[:, at] = grad
+            s_part = s_part + grad.astype(F32) * acc[0:PROMPT_PAD, at]
 
     def grad_block(j):
         rows = pl.ds(pl.multiple_of(j * COLS, COLS), COLS)
@@ -407,10 +431,12 @@
         rs_tx[way, step, t] = value.astype(BF)
         rs_copy(way, step, t).start()
 
-    block = grad_block(mod8(z + 4))
     for way in range(2):
-        for t in RS_LAST[way]:
-            rs_put(way, 0, t, block[:, 128 * t : 128 * t + 128])
+        first, count = RS_LAST[way][0], len(RS_LAST[way])
+        rows = pl.ds(pl.multiple_of(mod8(z + 4) * COLS + 128 * first, 128), 128 * count)
+        part = dot_t(gcat[0:PROMPT_SENT], w_all[rows, :])
+        for i in range(count):
+            rs_put(way, 0, first + i, part[:, 128 * i : 128 * i + 128])
     blocks = (grad_block(mod8(z + 3)), grad_block(mod8(z - 3)))
     for way in range(2):
         for t in RS_LAST[1 - way]:
@@ -424,12 +450,17 @@
     for h in range(HEADS):
         lanes = slice(HD * h, HD * h + HD)
         x = o_full[:, lanes]
-        head_row = lax.broadcasted_iota(jnp.int32, (ROWS_PAD, 128), 0)
-        outer = jnp.where(head_row < PROMPT, jnp.concatenate([x[TEXT:], x[:TEXT]], axis=0), pltpu.roll(x, PROMPT, 0))
+        outer = jnp.where(row < PROMPT, x, pltpu.roll(x, ROWS_PAD - (PROMPT_PAD - PROMPT), 0))
         outer = outer.astype(BF)
         for g in range(R_HIGH):
             ot_src[h * R_HIGH + g] = outer[R_ROWS * g : R_ROWS * g + R_ROWS]
     scatter_rows(ot_src, ot_mid, OT)
+
+    def relay_out():
+        @pl.when(there_r)
+        def _():
+            await_middle(ot_mid, OT)
+            relay(lambda s: ot_mid[inverse_slot[s]], ot_send, ot_dst, OT, mine_r)
 
     for t in (0, 1, 2):
         for way in range(2):
@@ -445,12 +476,8 @@
                 rs_copy(way, step - 1, t).wait_recv()
                 value = blocks[way][:, 128 * t : 128 * t + 128] + rs_rx[way, step - 1, t].astype(F32)
                 rs_put(way, step, t, value)
-        if step == 2:
-
-            @pl.when(there_r)
-            def _():
-                await_middle(ot_mid, OT)
-                relay(lambda s: ot_mid[inverse_slot[s]], ot_send, ot_dst, OT, mine_r)
+            if step == 3 and i == 1:
+                relay_out()
 
     own = grad_block(z)
     await_bytes(sx_all, sm_r.at[2], NZ - 1)
@@ -535,7 +562,6 @@
     vmem, dma, smem = pltpu.VMEM, pltpu.SemaphoreType.DMA, pltpu.SMEM
     anywhere = pl.BlockSpec(memory_space=pl.ANY)
     whole = pl.BlockSpec(memory_space=pltpu.VMEM)
-    scalars = pl.BlockSpec(memory_space=pltpu.SMEM)
     g_piece, r_piece = (G_ROWS, 128), (R_ROWS, 128)
     out_pieces, grad_pieces = pl.pallas_call(
         kernel,
@@ -543,10 +569,10 @@
             pltpu.VMEM((R_PIECES, *r_piece), BF),
             pltpu.VMEM((ND, *g_piece), BF),
         ),
-        in_specs=[scalars] * 3 + [anywhere, anywhere, whole] + [anywhere] * 6,
+        in_specs=[anywhere] * 12,
         out_specs=(whole, whole),
         scratch_shapes=[
-            smem((ND,), jnp.int32), smem((ND,), jnp.int32),
+            *[smem((ND,), jnp.int32)] * 5, vmem((NZ, 1, COLS), F32),
             vmem((NZ, TEXT, COLS), BF), vmem((NZ, PROMPT_PAD, COLS), BF), vmem((PROMPT, COLS), BF),
             vmem((ROWS, WIDTH), BF), vmem((NZ * COLS, ALL), BF),
             vmem((ROWS_PAD, HD), F32), vmem((ROWS_PAD, HD), F32),
@@ -558,11 +584,11 @@
             vmem((R_PIECES, *r_piece), BF), vmem((ND, *r_piece), BF), vmem((ND, *r_piece), BF), vmem((R_PIECES, *r_piece), BF),
             vmem((R_PIECES, *r_piece), BF), vmem((ND, *r_piece), BF), vmem((ND, *r_piece), BF),
             vmem((ND, *g_piece), BF), vmem((ND, *g_piece), BF), vmem((ND, *g_piece), BF), vmem((ND, *g_piece), F32),
-            vmem((ROWS_PAD, WIDTH), F32), vmem((TEXT, WIDTH), BF), vmem((PROMPT_PAD, WIDTH), BF),
+            vmem((ROWS_PAD, WIDTH), F32), vmem((ROWS_PAD, WIDTH), BF),
             vmem((ROWS_PAD, WIDTH), F32), vmem((PROMPT_PAD, ALL), BF),
             vmem((2, TILES, PROMPT_SENT, 128), F32),
             vmem((2, 4, TILES, PROMPT_SENT, 128), BF), vmem((2, 4, TILES, PROMPT_SENT, 128), BF),
-            dma((8,)), dma((2, 4, len(SUBS))), dma((2, 4, len(SUBS))), dma((2, 4, TILES)), dma((2, 4, TILES)),
+            dma((12,)), dma((2, 4, len(SUBS))), dma((2, 4, len(SUBS))), dma((2, 4, TILES)), dma((2, 4, TILES)),
             dma((3,)), dma((3,)), dma((5, 2)), dma((5, 2)),
         ],
         compiler_params=pltpu.CompilerParams(

time: 83.6 us -> 80.1 us (0.958)
  Pallas kernels: 82.8 us -> 79.4 us
    pallas_call x1, Pallas kernels: 81.9 us -> 78.5 us  [on_device(): pl.pallas_call(kernel, out_shape=(pltpu.VMEM((R_PIECES, *r_piece), BF), p...]
where the time goes in v3:
time: 80.1 us; the launch traced here: 80 us
  Pallas kernels  79.4 us (99%)
    pallas_call x1, Pallas kernels, on_device(): pl.pallas_call(kernel, out_shape=(pltpu.VMEM((R_PIECES, *r_piece), BF), p...  78.5 us

profile of v3, /device:TPU:1, one launch (start us, length us, event | category | flops | bytes accessed | tf_op | source)
XLA Modules:
  0.0 80.0 jit_solution(11749966953605733361)
XLA Ops:
  0.6 78.5 %shard_map.131 = (bf16[27,40,128]{2,1,0:T(8,128)(2,1)S(1)}, bf16[32,16,128]{2,1,0:T(8,128)(2,1)S(1)}) custom-call(s32[32]{0:T(128)} %task_hbm.1, s32[32]{0:T(128)} %lengths_hbm.1, s32[32]{0:T(128)} %slot_hbm.1, bf16[1,256,640]{2,1,0:T(8,128)(2,1)} %text_hbm.1, bf16[1,100,640]{2,1,0:T(8,128)(2,1)} %prompts_hbm.1, f32[8,1,640]{2,1,0:T(1,128)} %bitcast.2, ...), custom_call_target="tpu_custom_call" | custom-call | tf_op jit(solution)/shard_map/pallas_call | solution.py:566
  79.2 0.9 %shard_map.132 = (bf16[1,356,384]{2,1,0:T(8,128)(2,1)}, f32[100,1,640]{2,1,0:T(1,128)}) custom-call(bf16[27,40,128]{2,1,0:T(8,128)(2,1)S(1)} %get-tuple-element.6.ot_ref, bf16[32,16,128]{2,1,0:T(8,128)(2,1)S(1)} %get-tuple-element.7.gr_ref), custom_call_target="tpu_custom_call" | custom-call | tf_op jit(solution)/shard_map/pallas_call | solution.py:601

commit v4 on v3

--- a/solution.py
+++ b/solution.py
@@ -132,12 +132,25 @@
             mid[d] = src[p]
 
     def scatter_rows(src, mid, which):
+        first = jnp.minimum(mine_r, R_PIECES - 1)
+
+        def send_piece(p):
+            m = lax.div(p * ND, R_PIECES)
+            remote(src.at[p], mid.at[d], a2_s.at[which, 0], a2_r.at[which, 0], {"dp": m}).start()
+
         def body(i, carry):
-            p = lax.rem(d + i, R_PIECES)
-            scatter_one(src, mid, which, p, lax.div(p * ND, R_PIECES))
+            send_piece(lax.rem(first + i, R_PIECES))
             return carry
 
-        lax.fori_loop(0, R_PIECES, body, 0)
+        lax.fori_loop(1, R_PIECES, body, 0)
+
+        @pl.when(there_r)
+        def _():
+            mid[d] = src[first]
+
+        @pl.when(jnp.logical_not(there_r))
+        def _():
+            send_piece(first)
 
     def scatter_all(src, mid, which):
         def body(i, carry):
@@ -235,11 +248,11 @@
             lanes = slice(128 * t, 128 * t + 128)
             nb[0:PROMPT_PAD, lanes] = (prm_all[c, :, lanes].astype(F32) * inv_p[...] * gain[c, :, lanes]).astype(BF)
 
-    def multiply(c):
+    def multiply(c, which=slice(0, ROWS_PAD)):
         rows = pl.ds(pl.multiple_of(c * COLS, COLS), COLS)
         for n in range(3):
             wide = slice(WIDTH * n, WIDTH * n + WIDTH)
-            acc[:, wide] += dot(nb[...], w_all[rows, wide])
+            acc[which, wide] += dot(nb[which], w_all[rows, wide])
 
     def project(c):
         normed_text(c)
@@ -360,9 +373,10 @@
 
     ring_step(4, TEXT_ORDER)
     normed_text(mod8(z + 4))
+    multiply(mod8(z + 4), slice(PROMPT_PAD, ROWS_PAD))
     ring_step(4, PROMPT_ORDER)
     normed_prompts(mod8(z + 4))
-    multiply(mod8(z + 4))
+    multiply(mod8(z + 4), slice(0, PROMPT_PAD))
 
     score_scale = 1.0 / math.sqrt(HD)
     cos_all, sin_all = cos_t[...], sin_t[...]
@@ -447,6 +461,13 @@
     sx_all[z] = lane_sums(s_part, PROMPT_PAD)
     send_small(sx_all, 2)
 
+    blocks = (grad_block(mod8(z + 2)), grad_block(mod8(z - 2)))
+    for t in (0, 1, 2):
+        for way in range(2):
+            if t < len(RS_LAST[way]):
+                tile = RS_LAST[way][t]
+                rs_copy(way, 0, tile).wait_recv()
+                rs_put(way, 1, tile, rs_own[way, tile] + rs_rx[way, 0, tile].astype(F32))
     for h in range(HEADS):
         lanes = slice(HD * h, HD * h + HD)
         x = o_full[:, lanes]
@@ -456,28 +477,19 @@
             ot_src[h * R_HIGH + g] = outer[R_ROWS * g : R_ROWS * g + R_ROWS]
     scatter_rows(ot_src, ot_mid, OT)
 
-    def relay_out():
-        @pl.when(there_r)
-        def _():
-            await_middle(ot_mid, OT)
-            relay(lambda s: ot_mid[inverse_slot[s]], ot_send, ot_dst, OT, mine_r)
-
-    for t in (0, 1, 2):
-        for way in range(2):
-            if t < len(RS_LAST[way]):
-                tile = RS_LAST[way][t]
-                rs_copy(way, 0, tile).wait_recv()
-                rs_put(way, 1, tile, rs_own[way, tile] + rs_rx[way, 0, tile].astype(F32))
     for step in (2, 3):
-        blocks = (grad_block(mod8(z + 4 - step)), grad_block(mod8(z - 4 + step)))
+        if step == 3:
+            blocks = (grad_block(mod8(z + 1)), grad_block(mod8(z - 1)))
         for i in range(TILES):
             for way in range(2):
                 t = RS_ORDER[way][i]
                 rs_copy(way, step - 1, t).wait_recv()
                 value = blocks[way][:, 128 * t : 128 * t + 128] + rs_rx[way, step - 1, t].astype(F32)
                 rs_put(way, step, t, value)
-            if step == 3 and i == 1:
-                relay_out()
+    @pl.when(there_r)
+    def _():
+        await_middle(ot_mid, OT)
+        relay(lambda s: ot_mid[inverse_slot[s]], ot_send, ot_dst, OT, mine_r)
 
     own = grad_block(z)
     await_bytes(sx_all, sm_r.at[2], NZ - 1)

time: 80.1 us -> 80 us (level)
  no operation moved by 1% of the time
where the time goes in v4:
time: 80 us; the launch traced here: 79.9 us
  Pallas kernels  79.2 us (99%)
    pallas_call x1, Pallas kernels, on_device(): pl.pallas_call(kernel, out_shape=(pltpu.VMEM((R_PIECES, *r_piece), BF), p...  78.3 us

profile of v4, /device:TPU:1, one launch (start us, length us, event | category | flops | bytes accessed | tf_op | source)
XLA Modules:
  0.0 79.9 jit_solution(15963272399193963439)
XLA Ops:
  0.6 78.3 %shard_map.131 = (bf16[27,40,128]{2,1,0:T(8,128)(2,1)S(1)}, bf16[32,16,128]{2,1,0:T(8,128)(2,1)S(1)}) custom-call(s32[32]{0:T(128)} %task_hbm.1, s32[32]{0:T(128)} %lengths_hbm.1, s32[32]{0:T(128)} %slot_hbm.1, bf16[1,256,640]{2,1,0:T(8,128)(2,1)} %text_hbm.1, bf16[1,100,640]{2,1,0:T(8,128)(2,1)} %prompts_hbm.1, f32[8,1,640]{2,1,0:T(1,128)} %bitcast.2, ...), custom_call_target="tpu_custom_call" | custom-call | tf_op jit(solution)/shard_map/pallas_call | solution.py:578
  79.0 0.9 %shard_map.132 = (bf16[1,356,384]{2,1,0:T(8,128)(2,1)}, f32[100,1,640]{2,1,0:T(1,128)}) custom-call(bf16[27,40,128]{2,1,0:T(8,128)(2,1)S(1)} %get-tuple-element.6.ot_ref, bf16[32,16,128]{2,1,0:T(8,128)(2,1)S(1)} %get-tuple-element.7.gr_ref), custom_call_target="tpu_custom_call" | custom-call | tf_op jit(solution)/shard_map/pallas_call | solution.py:613

commit v5 on v4

--- a/solution.py
+++ b/solution.py
@@ -113,6 +113,9 @@
     for load in loads:
         load.start()
 
+    def far_first(i):
+        return lax.rem(d + lax.rem(i + 15, ND - 1) + 1, ND)
+
     def remote(src, dst, s_sem, r_sem, where):
         return pltpu.make_async_remote_copy(
             src_ref=src, dst_ref=dst, send_sem=s_sem, recv_sem=r_sem, device_id=where, device_id_type=MESH
@@ -154,7 +157,7 @@
 
     def scatter_all(src, mid, which):
         def body(i, carry):
-            m = lax.rem(d + i, ND)
+            m = far_first(i)
             remote(src.at[m], mid.at[d], a2_s.at[which, 0], a2_r.at[which, 0], {"dp": m}).start()
             return carry
 
@@ -170,7 +173,7 @@
 
     def relay(value, send, dst, which, mine):
         def body(i, carry):
-            e = lax.rem(d + i, ND)
+            e = far_first(i)
             send[e] = value(e)
             remote(send.at[e], dst.at[mine], a2_s.at[which, 1], a2_r.at[which, 1], {"dp": e}).start()
             return carry
@@ -461,13 +464,6 @@
     sx_all[z] = lane_sums(s_part, PROMPT_PAD)
     send_small(sx_all, 2)
 
-    blocks = (grad_block(mod8(z + 2)), grad_block(mod8(z - 2)))
-    for t in (0, 1, 2):
-        for way in range(2):
-            if t < len(RS_LAST[way]):
-                tile = RS_LAST[way][t]
-                rs_copy(way, 0, tile).wait_recv()
-                rs_put(way, 1, tile, rs_own[way, tile] + rs_rx[way, 0, tile].astype(F32))
     for h in range(HEADS):
         lanes = slice(HD * h, HD * h + HD)
         x = o_full[:, lanes]
@@ -477,19 +473,26 @@
             ot_src[h * R_HIGH + g] = outer[R_ROWS * g : R_ROWS * g + R_ROWS]
     scatter_rows(ot_src, ot_mid, OT)
 
+    for t in (0, 1, 2):
+        for way in range(2):
+            if t < len(RS_LAST[way]):
+                tile = RS_LAST[way][t]
+                rs_copy(way, 0, tile).wait_recv()
+                rs_put(way, 1, tile, rs_own[way, tile] + rs_rx[way, 0, tile].astype(F32))
     for step in (2, 3):
-        if step == 3:
-            blocks = (grad_block(mod8(z + 1)), grad_block(mod8(z - 1)))
+        blocks = (grad_block(mod8(z + 4 - step)), grad_block(mod8(z - 4 + step)))
         for i in range(TILES):
             for way in range(2):
                 t = RS_ORDER[way][i]
                 rs_copy(way, step - 1, t).wait_recv()
                 value = blocks[way][:, 128 * t : 128 * t + 128] + rs_rx[way, step - 1, t].astype(F32)
                 rs_put(way, step, t, value)
-    @pl.when(there_r)
-    def _():
-        await_middle(ot_mid, OT)
-        relay(lambda s: ot_mid[inverse_slot[s]], ot_send, ot_dst, OT, mine_r)
+            if step == 3 and i == 1:
+
+                @pl.when(there_r)
+                def _():
+                    await_middle(ot_mid, OT)
+                    relay(lambda s: ot_mid[inverse_slot[s]], ot_send, ot_dst, OT, mine_r)
 
     own = grad_block(z)
     await_bytes(sx_all, sm_r.at[2], NZ - 1)

time: 80 us -> 80.4 us (level)
  no operation moved by 1% of the time
where the time goes in v5:
time: 80.4 us; the launch traced here: 80.3 us
  Pallas kernels  79.6 us (99%)
    pallas_call x1, Pallas kernels, on_device(): pl.pallas_call(kernel, out_shape=(pltpu.VMEM((R_PIECES, *r_piece), BF), p...  78.7 us

profile of v5, /device:TPU:1, one launch (start us, length us, event | category | flops | bytes accessed | tf_op | source)
XLA Modules:
  0.0 80.3 jit_solution(4984758926438935786)
XLA Ops:
  0.6 78.7 %shard_map.131 = (bf16[27,40,128]{2,1,0:T(8,128)(2,1)S(1)}, bf16[32,16,128]{2,1,0:T(8,128)(2,1)S(1)}) custom-call(s32[32]{0:T(128)} %task_hbm.1, s32[32]{0:T(128)} %lengths_hbm.1, s32[32]{0:T(128)} %slot_hbm.1, bf16[1,256,640]{2,1,0:T(8,128)(2,1)} %text_hbm.1, bf16[1,100,640]{2,1,0:T(8,128)(2,1)} %prompts_hbm.1, f32[8,1,640]{2,1,0:T(1,128)} %bitcast.2, ...), custom_call_target="tpu_custom_call" | custom-call | tf_op jit(solution)/shard_map/pallas_call | solution.py:581
  79.4 0.9 %shard_map.132 = (bf16[1,356,384]{2,1,0:T(8,128)(2,1)}, f32[100,1,640]{2,1,0:T(1,128)}) custom-call(bf16[27,40,128]{2,1,0:T(8,128)(2,1)S(1)} %get-tuple-element.6.ot_ref, bf16[32,16,128]{2,1,0:T(8,128)(2,1)S(1)} %get-tuple-element.7.gr_ref), custom_call_target="tpu_custom_call" | custom-call | tf_op jit(solution)/shard_map/pallas_call | solution.py:616

commit v6 on v4

--- a/solution.py
+++ b/solution.py
@@ -41,6 +41,7 @@
 PROMPT_ORDER = ((4, 5), (5, 4))
 RS_LAST = ((0, 1, 2), (3, 4))
 RS_ORDER = ((3, 4, 0, 1, 2), (0, 1, 2, 3, 4))
+FINAL_ORDER = (0, 1, 3, 4, 2)
 
 
 def rope_constants():
@@ -122,14 +123,10 @@
     there_r = jnp.logical_and(mine_r < R_PIECES, lax.div(mine_r * ND, R_PIECES) == d)
     PP, CT, OT, GR, SP = range(5)
 
-    def scatter_one(src, mid, which, p, m):
-        @pl.when(m != d)
+    def scatter_grad(p):
+        @pl.when(d != p)
         def _():
-            remote(src.at[p], mid.at[d], a2_s.at[which, 0], a2_r.at[which, 0], {"dp": m}).start()
-
-        @pl.when(m == d)
-        def _():
-            mid[d] = src[p]
+            remote(gr_src.at[p], gr_mid.at[d], a2_s.at[GR, 0], a2_r.at[GR, 0], {"dp": p}).start()
 
     def scatter_rows(src, mid, which):
         first = jnp.minimum(mine_r, R_PIECES - 1)
@@ -496,8 +493,8 @@
     s_col[...] = jnp.broadcast_to(total_of(sx_all) * (1.0 / (NZ * COLS)), (128, PROMPT_PAD)).T
     inv = inv_p[0:PROMPT_SENT]
     second = inv * inv * s_col[0:PROMPT_SENT]
-    ends = []
-    for t in range(TILES):
+    ends = [None] * TILES
+    for t in FINAL_ORDER:
         lanes = slice(128 * t, 128 * t + 128)
         value = own[:, lanes]
         for way in range(2):
@@ -508,12 +505,13 @@
         for g in range(G_HIGH):
             p = t * G_HIGH + g
             gr_src[p] = low[G_ROWS * g : G_ROWS * g + G_ROWS]
-            scatter_one(gr_src, gr_mid, GR, p, p)
-        ends.append(value[96:100])
+            scatter_grad(p)
+        ends[t] = value[96:100]
     first, second = tail_rows(ends)
     for p, value in ((30, first), (31, second)):
         gr_src[p] = value.astype(BF)
-        scatter_one(gr_src, gr_mid, GR, p, p)
+        scatter_grad(p)
+    gr_mid[d] = gr_src[d]
     await_middle(gr_mid, GR)
     before = jnp.zeros((G_ROWS, 128), F32)
     for e in range(ND):

time: 80 us -> 79.3 us (level)
  no operation moved by 1% of the time
where the time goes in v6:
time: 79.3 us; the launch traced here: 79.2 us
  Pallas kernels  78.5 us (99%)
    pallas_call x1, Pallas kernels, on_device(): pl.pallas_call(kernel, out_shape=(pltpu.VMEM((R_PIECES, *r_piece), BF), p...  77.6 us

profile of v6, /device:TPU:1, one launch (start us, length us, event | category | flops | bytes accessed | tf_op | source)
XLA Modules:
  0.0 79.2 jit_solution(10659000834751997186)
XLA Ops:
  0.6 77.6 %shard_map.131 = (bf16[27,40,128]{2,1,0:T(8,128)(2,1)S(1)}, bf16[32,16,128]{2,1,0:T(8,128)(2,1)S(1)}) custom-call(s32[32]{0:T(128)} %task_hbm.1, s32[32]{0:T(128)} %lengths_hbm.1, s32[32]{0:T(128)} %slot_hbm.1, bf16[1,256,640]{2,1,0:T(8,128)(2,1)} %text_hbm.1, bf16[1,100,640]{2,1,0:T(8,128)(2,1)} %prompts_hbm.1, f32[8,1,640]{2,1,0:T(1,128)} %bitcast.2, ...), custom_call_target="tpu_custom_call" | custom-call | tf_op jit(solution)/shard_map/pallas_call | solution.py:576
  78.3 0.9 %shard_map.132 = (bf16[1,356,384]{2,1,0:T(8,128)(2,1)}, f32[100,1,640]{2,1,0:T(1,128)}) custom-call(bf16[27,40,128]{2,1,0:T(8,128)(2,1)S(1)} %get-tuple-element.6.ot_ref, bf16[32,16,128]{2,1,0:T(8,128)(2,1)S(1)} %get-tuple-element.7.gr_ref), custom_call_target="tpu_custom_call" | custom-call | tf_op jit(solution)/shard_map/pallas_call | solution.py:611

commit v7 on v6

--- a/solution.py
+++ b/solution.py
@@ -41,6 +41,7 @@
 PROMPT_ORDER = ((4, 5), (5, 4))
 RS_LAST = ((0, 1, 2), (3, 4))
 RS_ORDER = ((3, 4, 0, 1, 2), (0, 1, 2, 3, 4))
+HALVES = ((0, 48), (48, 104))
 FINAL_ORDER = (0, 1, 3, 4, 2)
 
 
@@ -432,15 +433,23 @@
         rows = pl.ds(pl.multiple_of(j * COLS, COLS), COLS)
         return dot_t(gcat[0:PROMPT_SENT], w_all[rows, :])
 
-    def rs_copy(way, step, t):
+    def rs_copy(way, step, t, half):
+        rows = slice(*HALVES[half])
         return remote(
-            rs_tx.at[way, step, t], rs_rx.at[way, step, t], rs_s.at[way, step, t], rs_r.at[way, step, t],
+            rs_tx.at[way, step, t, rows], rs_rx.at[way, step, t, rows],
+            rs_s.at[way, step, t, half], rs_r.at[way, step, t, half],
             {"tensor": mod8(z + SIGN[way])},
         )
 
-    def rs_put(way, step, t, value):
-        rs_tx[way, step, t] = value.astype(BF)
-        rs_copy(way, step, t).start()
+    def rs_put(way, step, t, value, add=False):
+        for half in range(2):
+            rows = slice(*HALVES[half])
+            now = value[rows]
+            if add:
+                rs_copy(way, step - 1, t, half).wait_recv()
+                now = now + rs_rx[way, step - 1, t, rows].astype(F32)
+            rs_tx[way, step, t, rows] = now.astype(BF)
+            rs_copy(way, step, t, half).start()
 
     for way in range(2):
         first, count = RS_LAST[way][0], len(RS_LAST[way])
@@ -463,8 +472,7 @@
         for way in range(2):
             if t < len(RS_LAST[way]):
                 tile = RS_LAST[way][t]
-                rs_copy(way, 0, tile).wait_recv()
-                rs_put(way, 1, tile, rs_own[way, tile] + rs_rx[way, 0, tile].astype(F32))
+                rs_put(way, 1, tile, rs_own[way, tile], add=True)
     for h in range(HEADS):
         lanes = slice(HD * h, HD * h + HD)
         x = o_full[:, lanes]
@@ -480,9 +488,7 @@
         for i in range(TILES):
             for way in range(2):
                 t = RS_ORDER[way][i]
-                rs_copy(way, step - 1, t).wait_recv()
-                value = blocks[way][:, 128 * t : 128 * t + 128] + rs_rx[way, step - 1, t].astype(F32)
-                rs_put(way, step, t, value)
+                rs_put(way, step, t, blocks[way][:, 128 * t : 128 * t + 128], add=True)
     @pl.when(there_r)
     def _():
         await_middle(ot_mid, OT)
@@ -498,7 +504,8 @@
         lanes = slice(128 * t, 128 * t + 128)
         value = own[:, lanes]
         for way in range(2):
-            rs_copy(way, 3, t).wait_recv()
+            for half in range(2):
+                rs_copy(way, 3, t, half).wait_recv()
             value = value + rs_rx[way, 3, t].astype(F32)
         value = inv * (value * gain[z, :, lanes]) - prm_all[z, 0:PROMPT_SENT, lanes].astype(F32) * second
         low = value.astype(BF)
@@ -551,7 +558,8 @@
         for step in range(4):
             for t in range(TILES):
                 if step > 0 or t in RS_LAST[way]:
-                    rs_copy(way, step, t).wait_send()
+                    for half in range(2):
+                        rs_copy(way, step, t, half).wait_send()
 
 
 def assemble(ot_ref, gr_ref, out_ref, pg_ref):
@@ -598,7 +606,7 @@
             vmem((ROWS_PAD, WIDTH), F32), vmem((PROMPT_PAD, ALL), BF),
             vmem((2, TILES, PROMPT_SENT, 128), F32),
             vmem((2, 4, TILES, PROMPT_SENT, 128), BF), vmem((2, 4, TILES, PROMPT_SENT, 128), BF),
-            dma((12,)), dma((2, 4, len(SUBS))), dma((2, 4, len(SUBS))), dma((2, 4, TILES)), dma((2, 4, TILES)),
+            dma((12,)), dma((2, 4, len(SUBS))), dma((2, 4, len(SUBS))), dma((2, 4, TILES, 2)), dma((2, 4, TILES, 2)),
             dma((3,)), dma((3,)), dma((5, 2)), dma((5, 2)),
         ],
         compiler_params=pltpu.CompilerParams(

time: 79.3 us -> 79.7 us (level)
  no operation moved by 1% of the time
where the time goes in v7:
time: 79.7 us; the launch traced here: 79.6 us
  Pallas kernels  79 us (99%)
    pallas_call x1, Pallas kernels, on_device(): pl.pallas_call(kernel, out_shape=(pltpu.VMEM((R_PIECES, *r_piece), BF), p...  78.1 us

profile of v7, /device:TPU:1, one launch (start us, length us, event | category | flops | bytes accessed | tf_op | source)
XLA Modules:
  0.0 79.6 jit_solution(6120903636691495536)
XLA Ops:
  0.6 78.1 %shard_map.131 = (bf16[27,40,128]{2,1,0:T(8,128)(2,1)S(1)}, bf16[32,16,128]{2,1,0:T(8,128)(2,1)S(1)}) custom-call(s32[32]{0:T(128)} %task_hbm.1, s32[32]{0:T(128)} %lengths_hbm.1, s32[32]{0:T(128)} %slot_hbm.1, bf16[1,256,640]{2,1,0:T(8,128)(2,1)} %text_hbm.1, bf16[1,100,640]{2,1,0:T(8,128)(2,1)} %prompts_hbm.1, f32[8,1,640]{2,1,0:T(1,128)} %bitcast.2, ...), custom_call_target="tpu_custom_call" | custom-call | tf_op jit(solution)/shard_map/pallas_call | solution.py:584
  78.7 0.9 %shard_map.132 = (bf16[1,356,384]{2,1,0:T(8,128)(2,1)}, f32[100,1,640]{2,1,0:T(1,128)}) custom-call(bf16[27,40,128]{2,1,0:T(8,128)(2,1)S(1)} %get-tuple-element.6.ot_ref, bf16[32,16,128]{2,1,0:T(8,128)(2,1)S(1)} %get-tuple-element.7.gr_ref), custom_call_target="tpu_custom_call" | custom-call | tf_op jit(solution)/shard_map/pallas_call | solution.py:619
